TPU v7x, 32 devices: a whole 2x2x4 slice. The times are simulated.
32 devices in a mesh: dp: 8 (over z, y), tensor: 4 (over x, core).
Axes of the slice: x: 2, y: 2, z: 4, core: 2. Of those that a mesh axis runs over, the one named last changes fastest.
Arguments:
- tokens: bfloat16 [32768, 1024], P(('dp', 'tensor')), may hold values from -6 to 6
- segments: int32 [64, 512], P(('dp', 'tensor')), may hold values from 0 to 1, as said below
- lengths: int32 [64], P(('dp', 'tensor')), may hold values from 128 to 512, as said below
- type_table: bfloat16 [2, 1024], replicated, may hold values from -3 to 3
- attn_weight: bfloat16 [3145728], P(('dp', 'tensor')), may hold values from -0.1875 to 0.1875
- out_weight: bfloat16 [1048576], P(('dp', 'tensor')), may hold values from -0.75 to 0.75
- ffn_in_weight: bfloat16 [1024, 4096], P('dp', 'tensor'), may hold values from -0.1875 to 0.1875
- ffn_out_weight: bfloat16 [4096, 1024], P('tensor', 'dp'), may hold values from -0.125 to 0.125
- attn_bias: bfloat16 [3, 1024], replicated, may hold values from -3 to 3
- ffn_bias_in: bfloat16 [4096], replicated, may hold values from -3 to 3
- ffn_bias_out: bfloat16 [1024], replicated, may hold values from -3 to 3
- norm_gain: bfloat16 [2, 1024], replicated, may hold values from 0.099609375 to 1.8984375
- norm_shift: bfloat16 [2, 1024], replicated, may hold values from -3 to 3
- cotangent: bfloat16 [32768, 1024], P(('dp', 'tensor')), may hold values from -6 to 6
Outputs:
- output: bfloat16 [32768, 1024], P(('dp', 'tensor'))
- grad_input: bfloat16 [32768, 1024], P(('dp', 'tensor'))
- attn_bias_grad: float32 [3, 1024], replicated
- ffn_bias_in_grad: float32 [4096], replicated
- ffn_bias_out_grad: float32 [1024], replicated
- norm_gain_grad: float32 [2, 1024], replicated
- norm_shift_grad: float32 [2, 1024], replicated
Inputs may be any that keep to these rules, and one draw needn't show every extreme that they name: `lengths`: the valid tokens of a sequence are its first ones; in every draw some sequence has all 512 valid. `segments`: segment id 0 up to and including a separator at position 1 to length - 2, 1 after it up to the sequence's length, 0 on padding.
All inputs are finite; a program needn't handle non-finite values.
Results may differ from a plain program's by a relative error of at most 0.015.
Values may be sent and summed in bfloat16 or wider, within the bound.
A program may use at most 192 MiB of HBM per device.

v0:
```python
from functools import partial
import math

import jax
import jax.numpy as jnp
from jax import lax
from jax.sharding import PartitionSpec as P

HEADS = 16
HEAD = 64


def matmul(left_side, right_side):
    return jnp.dot(left_side, right_side, preferred_element_type=jnp.float32)


def matmul_t(left_side, right_side):
    return lax.dot_general(
        left_side, right_side, (((1,), (1,)), ((), ())), preferred_element_type=jnp.float32
    )


def norm_forward(residual, gain_row, shift_row):
    row_mean = jnp.mean(residual, axis=-1, keepdims=True)
    centered = residual - row_mean
    inverse = lax.rsqrt(jnp.mean(centered * centered, axis=-1, keepdims=True) + 1e-12)
    normed = centered * inverse
    return (normed * gain_row + shift_row, normed, inverse)


def norm_backward(upstream, normed, inverse, gain_row):
    scaled = upstream * gain_row
    inner = (
        scaled
        - jnp.mean(scaled, axis=-1, keepdims=True)
        - normed * jnp.mean(scaled * normed, axis=-1, keepdims=True)
    )
    return (inner * inverse, jnp.sum(upstream * normed, axis=0), jnp.sum(upstream, axis=0))


def gelu_slope(preact):
    normal_cdf = 0.5 * (1.0 + jax.scipy.special.erf(preact * 0.7071067811865476))
    normal_pdf = jnp.exp(-0.5 * preact * preact) * 0.3989422804014327
    return normal_cdf + preact * normal_pdf


def score_block(queries, key_rows, key_valid, score_scale):
    scores = (
        jnp.einsum("qhd,khd->hqk", queries, key_rows, preferred_element_type=jnp.float32)
        * score_scale
    )
    return jnp.where(key_valid[None, None, :], scores, -1000000000.0)


def context_block(block_items, score_scale):
    queries, key_rows, value_rows, key_valid = block_items
    masked = score_block(queries, key_rows, key_valid, score_scale)
    row_max = jnp.max(masked, axis=-1, keepdims=True)
    log_total = row_max + jnp.log(jnp.sum(jnp.exp(masked - row_max), axis=-1, keepdims=True))
    attn_prob = jnp.exp(masked - log_total)
    context = jnp.einsum(
        "hqk,khd->qhd",
        attn_prob.astype(jnp.bfloat16),
        value_rows,
        preferred_element_type=jnp.float32,
    )
    return (context.astype(jnp.bfloat16), log_total)


def gradient_block(block_items, score_scale):
    queries, key_rows, value_rows, key_valid, log_total, d_context = block_items
    masked = score_block(queries, key_rows, key_valid, score_scale)
    attn_prob = jnp.exp(masked - log_total)
    d_prob = jnp.einsum("qhd,khd->hqk", d_context, value_rows, preferred_element_type=jnp.float32)
    d_values = jnp.einsum(
        "hqk,qhd->khd",
        attn_prob.astype(jnp.bfloat16),
        d_context,
        preferred_element_type=jnp.float32,
    )
    row_dot = jnp.sum(d_prob * attn_prob, axis=-1, keepdims=True)
    d_scores = (attn_prob * (d_prob - row_dot)).astype(jnp.bfloat16)
    d_queries = (
        jnp.einsum("hqk,khd->qhd", d_scores, key_rows, preferred_element_type=jnp.float32)
        * score_scale
    )
    d_keys = (
        jnp.einsum("hqk,qhd->khd", d_scores, queries, preferred_element_type=jnp.float32)
        * score_scale
    )
    return (
        d_queries.astype(jnp.bfloat16),
        d_keys.astype(jnp.bfloat16),
        d_values.astype(jnp.bfloat16),
    )


def per_device(
    tokens,
    segments,
    lengths,
    type_table,
    attn_weight,
    out_weight,
    ffn_in_weight,
    ffn_out_weight,
    attn_bias,
    ffn_bias_in,
    ffn_bias_out,
    norm_gain,
    norm_shift,
    cotangent,
):
    tok_rows, model_width = tokens.shape
    seq_count, seq_len = segments.shape
    score_scale = 1.0 / math.sqrt(HEAD)
    bias_attn = attn_bias.astype(jnp.float32)
    bias_first = ffn_bias_in.astype(jnp.float32)
    bias_second = ffn_bias_out.astype(jnp.float32)
    gain_rows = norm_gain.astype(jnp.float32)
    shift_rows = norm_shift.astype(jnp.float32)
    qkv_flat, out_flat = (
        lax.all_gather(attn_weight, ("dp", "tensor"), axis=0, tiled=True),
        lax.all_gather(out_weight, ("dp", "tensor"), axis=0, tiled=True),
    )
    projections = qkv_flat.reshape(3, model_width, model_width)
    out_proj = out_flat.reshape(model_width, model_width)
    w_first, w_second = (
        lax.all_gather(ffn_in_weight, "dp", axis=0, tiled=True),
        lax.all_gather(ffn_out_weight, "dp", axis=1, tiled=True),
    )
    w_first, w_second = (
        lax.all_gather(w_first, "tensor", axis=1, tiled=True),
        lax.all_gather(w_second, "tensor", axis=0, tiled=True),
    )
    table_rows = type_table.astype(jnp.float32)
    type_rows = jnp.where(
        (segments.reshape(-1) == 1)[:, None], table_rows[1][None, :], table_rows[0][None, :]
    )
    block_input = tokens.astype(jnp.float32) + type_rows
    lowered = block_input.astype(jnp.bfloat16)
    projected = jnp.einsum("td,mde->mte", lowered, projections, preferred_element_type=jnp.float32)
    queries = (projected[0] + bias_attn[0]).astype(jnp.bfloat16)
    key_rows = projected[1].astype(jnp.bfloat16)
    value_rows = (projected[2] + bias_attn[1]).astype(jnp.bfloat16)
    head_shape = (seq_count, seq_len, HEADS, HEAD)
    query_heads = queries.reshape(head_shape)
    key_heads = key_rows.reshape(head_shape)
    value_heads = value_rows.reshape(head_shape)
    key_valid = jnp.arange(seq_len, dtype=jnp.int32)[None, :] < lengths[:, None]
    context, log_total = lax.map(
        partial(context_block, score_scale=score_scale),
        (query_heads, key_heads, value_heads, key_valid),
    )
    context = context.reshape(tok_rows, model_width)
    attn_out = matmul(context, out_proj) + bias_attn[2]
    middle, normed_one, inverse_one = norm_forward(
        block_input + attn_out, gain_rows[0], shift_rows[0]
    )
    middle_low = middle.astype(jnp.bfloat16)
    preact = matmul(middle_low, w_first) + bias_first
    hidden = jax.nn.gelu(preact, approximate=False).astype(jnp.bfloat16)
    ffn_out = matmul(hidden, w_second) + bias_second
    output_rows, normed_two, inverse_two = norm_forward(
        middle + ffn_out, gain_rows[1], shift_rows[1]
    )
    output = output_rows.astype(jnp.bfloat16)
    qkv_again, out_again = (
        lax.all_gather(attn_weight, ("dp", "tensor"), axis=0, tiled=True),
        lax.all_gather(out_weight, ("dp", "tensor"), axis=0, tiled=True),
    )
    projections = qkv_again.reshape(3, model_width, model_width)
    out_proj = out_again.reshape(model_width, model_width)
    w_first, w_second = (
        lax.all_gather(ffn_in_weight, "dp", axis=0, tiled=True),
        lax.all_gather(ffn_out_weight, "dp", axis=1, tiled=True),
    )
    w_first, w_second = (
        lax.all_gather(w_first, "tensor", axis=1, tiled=True),
        lax.all_gather(w_second, "tensor", axis=0, tiled=True),
    )
    d_second_sum, gain_two_grad, shift_two_grad = norm_backward(
        cotangent.astype(jnp.float32), normed_two, inverse_two, gain_rows[1]
    )
    d_ffn = d_second_sum.astype(jnp.bfloat16)
    bias_out_grad = jnp.sum(d_ffn.astype(jnp.float32), axis=0)
    d_preact = (matmul_t(d_ffn, w_second) * gelu_slope(preact)).astype(jnp.bfloat16)
    bias_in_grad = jnp.sum(d_preact.astype(jnp.float32), axis=0)
    d_middle_ffn = matmul_t(d_preact, w_first)
    d_middle = d_second_sum + d_middle_ffn
    d_first_sum, gain_one_grad, shift_one_grad = norm_backward(
        d_middle, normed_one, inverse_one, gain_rows[0]
    )
    d_attn = d_first_sum.astype(jnp.bfloat16)
    bias_o_grad = jnp.sum(d_attn.astype(jnp.float32), axis=0)
    d_context = matmul_t(d_attn, out_proj).astype(jnp.bfloat16).reshape(head_shape)
    d_queries, d_keys, d_values = lax.map(
        partial(gradient_block, score_scale=score_scale),
        (query_heads, key_heads, value_heads, key_valid, log_total, d_context),
    )
    d_queries = d_queries.reshape(tok_rows, model_width)
    d_keys = d_keys.reshape(tok_rows, model_width)
    d_values = d_values.reshape(tok_rows, model_width)
    bias_q_grad = jnp.sum(d_queries.astype(jnp.float32), axis=0)
    bias_v_grad = jnp.sum(d_values.astype(jnp.float32), axis=0)
    stacked = jnp.stack([d_queries, d_keys, d_values])
    d_input = d_first_sum + jnp.einsum(
        "mte,mde->td", stacked, projections, preferred_element_type=jnp.float32
    )
    grad_input = d_input.astype(jnp.bfloat16)
    attn_grad = jnp.stack([bias_q_grad, bias_v_grad, bias_o_grad])
    gain_grad = jnp.stack([gain_one_grad, gain_two_grad])
    shift_grad = jnp.stack([shift_one_grad, shift_two_grad])
    attn_grad, bias_in_grad, bias_out_grad, gain_grad, shift_grad = lax.psum(
        (attn_grad, bias_in_grad, bias_out_grad, gain_grad, shift_grad), ("dp", "tensor")
    )
    return (output, grad_input, attn_grad, bias_in_grad, bias_out_grad, gain_grad, shift_grad)


def solution(mesh):
    in_specs = (
        P(("dp", "tensor"), None),
        P(("dp", "tensor"), None),
        P(("dp", "tensor")),
        P(),
        P(("dp", "tensor")),
        P(("dp", "tensor")),
        P("dp", "tensor"),
        P("tensor", "dp"),
        P(),
        P(),
        P(),
        P(),
        P(),
        P(("dp", "tensor"), None),
    )
    out_specs = (P(("dp", "tensor"), None), P(("dp", "tensor"), None), P(), P(), P(), P(), P())
    return jax.shard_map(
        per_device, mesh=mesh, in_specs=in_specs, out_specs=out_specs, check_vma=False
    )
```

profile of v0, /device:TPU:0, one launch (start us, length us, event | category | flops | bytes accessed | tf_op | source)
XLA Modules:
  0.0 693.1 jit_solution(5041062795089590468)
XLA Ops:
  10.0 51.9 %all-gather.11.cloned.1.call-done = bf16[1024,1024]{1,0:T(8,128)(2,1)} async-done(((bf16[128,1024]{1,0:T(8,128)(2,1)}), bf16[1024,1024]{1,0:T(8,128)(2,1)}) %all-gather.11.cloned.1.call-update) | async-done | bytes 2097168 | tf_op jit(solution)/shard_map/all_gather | solution.py:129
  67.5 3.9 copy.85
  72.7 40.2 %all-gather.15.cloned.1.call-done = bf16[1024,1024]{1,0:T(8,128)(2,1)} async-done(((bf16[1024,128]{1,0:T(8,128)(2,1)}), bf16[1024,1024]{1,0:T(8,128)(2,1)}) %all-gather.15.cloned.1.call-update) | async-done | bytes 2097168 | tf_op jit(solution)/shard_map/all_gather | solution.py:130
  113.0 57.3 %all-gather.9.cloned.1.call-done = bf16[1048576]{0:T(1024)(128)(2,1)} async-done(((bf16[32768]{0:T(1024)(128)(2,1)}), bf16[1048576]{0:T(1024)(128)(2,1)}) %all-gather.9.cloned.1.call-update) | async-done | bytes 2097168 | tf_op jit(solution)/shard_map/all_gather | solution.py:124
  170.2 4.1 reshape.135
  174.4 66.6 %all-gather.7.cloned.1.call-done = bf16[3145728]{0:T(1024)(128)(2,1)} async-done(((bf16[98304]{0:T(1024)(128)(2,1)}), bf16[3145728]{0:T(1024)(128)(2,1)}) %all-gather.7.cloned.1.call-update) | async-done | bytes 6291472 | tf_op jit(solution)/shard_map/all_gather | solution.py:123
  241.0 10.6 %reshape.133 = bf16[3,1024,1024]{2,1,0:T(8,128)(2,1)} reshape(bf16[3145728]{0:T(1024)(128)(2,1)} %all-gather.7.cloned.1.call-done) | data formatting | bytes 12582912 | tf_op jit(solution)/shard_map/reshape | solution.py:126
  251.5 11.7 %convolution_bitcast_fusion = f32[3,1024,1024]{2,1,0:T(8,128)S(1)} fusion(bf16[3,1024,1024]{2,1,0:T(8,128)(2,1)} %reshape.133, bf16[1024,1024]{0,1:T(8,128)(2,1)S(1)} %copy-done.22, f32[1024]{0:T(1024)S(1)} %bitcast.169, f32[1024]{0:T(1024)S(1)} %bitcast.167, pred[1024]{0:T(1024)(128)(4,1)S(1)} %eq.15), kind=kOutput, calls=%fused_computation.99 | convolution fusion | flops 6446645248 | bytes 20980736 | tf_op jit(solution)/shard_map/td,mde->mte/dot_general | solution.py:142
  263.5 4.1 fusion.135
  267.7 5.4 copy.77
  273.1 6.6 squeeze.34
  279.7 3.9 add_convert_fusion.2
  285.4 5.4 copy.78
  290.8 6.6 squeeze.35
  297.4 3.9 add_convert_fusion.1
  303.2 4.0 reshape.143
  307.2 4.9 copy.82
  313.7 28.0 %while.26 = (s32[]{:T(128)}, bf16[2,512,16,64]{1,3,2,0:T(8,128)(2,1)}, f32[2,16,512,1]{2,1,3,0:T(8,128)S(1)}, bf16[2,512,16,64]{1,3,2,0:T(8,128)(2,1)}, pred[2,5...) while((s32[]{:T(128)}, ...), condition=%wide.region_3.4_spmd, body=%wide.region_0.3_spmd.sunk | while | flops 1120395264 | bytes 63181432 | solution.py:151
  313.7 5.1 fusion.169
  322.7 4.8 fusion.170
  327.5 5.0 fusion.169
  336.4 4.8 fusion.170
  341.7 4.6 copy.83
  352.3 16.8 %fusion.90 = f32[1024,4096]{1,0:T(8,128)} fusion(bf16[1024,4096]{1,0:T(8,128)(2,1)} %all-gather.13.cloned.1.call-done, f32[1024,1024]{0,1:T(8,128)} %copy-done.11, f32[1024]{0:T(1024)S(1)} %bitcast.165, f32[1024]{0:T(1024)S(1)} %bitcast.156, f32[1024]{0:T(1024)S(1)} %add_rsqrt_fusion.1, f32[1024]{0:T(1024)S(1)} %broadcast_multiply_fusion.5), kind=kOutput, calls=%fused_computation.128 | convolution fusion | flops 8595177472 | bytes 29376512 | tf_op jit(solution)/shard_map/dot_general | solution.py:14
  369.2 51.3 %fusion.140 = (f32[1024]{0:T(1024)S(1)}, f32[1024,1024]{0,1:T(8,128)}) fusion(f32[1024]{0:T(1024)S(1)} %copy-done.47, bf16[4096,1024]{1,0:T(8,128)(2,1)} %all-gather.17.cloned.1.call-done, f32[1024,4096]{1,0:T(8,128)} %fusion.90, f32[4096]{0:T(1024)S(1)} %copy-done.40, f32[1024]{0:T(1024)S(1)} %bitcast.166, f32[1024]{0:T(1024)S(1)} %bitcast.157, ...), kind=kOutput, calls=%fused_computation.192 | convolution fusion | flops 8874097664 | bytes 33595392 | tf_op jit(solution)/shard_map/dot_general | solution.py:14
  425.0 22.0 %convert_reduce_fusion = (f32[4096]{0:T(1024)}, bf16[1024,4096]{1,0:T(8,128)(2,1)}) fusion(f32[1024,4096]{1,0:T(8,128)} %fusion.90, f32[4096]{0:T(1024)S(1)} %copy-done.40, bf16[4096,1024]{1,0:T(8,128)(2,1)} %all-gather.17.cloned.1.call-done, f32[1024]{0:T(1024)S(1)} %get-tuple-element.250, f32[1024]{0:T(1024)S(1)} %add_rsqrt_fusion, ...), kind=kOutput, calls=%fused_computation.70 | convolution fusion | flops 8653893632 | bytes 39899136 | tf_op jit(solution)/shard_map/dot_general | solution.py:18
  447.1 17.5 %multiply_reduce_fusion.1 = (f32[1024]{0:T(1024)}, f32[1024]{0:T(1024)S(1)}, f32[1024]{0:T(1024)S(1)}, f32[1024]{0:T(1024)}, f32[1024,1024]{0,1:T(8,128)S(1)}) fusion(f32[1024,1024]{0,1:T(8,128)} %copy-done.11, f32[1024]{0:T(1024)S(1)} %add_rsqrt_fusion.1, f32[1024]{0:T(1024)S(1)} %broadcast_multiply_fusion.5, f32[1024]{0:T(1024)S(1)} %bitcast.158, ...), kind=kOutput, calls=%fused_computation.107 | convolution fusion | flops 8608804864 | bytes 31506432 | tf_op jit(solution)/shard_map/dot_general | solution.py:18
  471.1 4.0 reshape.139
  475.1 5.4 copy.90
  485.2 93.9 %while.27 = (s32[]{:T(128)}, bf16[2,512,16,64]{1,3,2,0:T(8,128)(2,1)}, bf16[2,512,16,64]{1,3,2,0:T(8,128)(2,1)}, bf16[2,512,16,64]{1,3,2,0:T(8,128)(2,1)}, bf16[...) while((s32[]{:T(128)}, ...), condition=%wide.region_14.15_spmd, body=%wide.region_12.14_spmd.sunk | while | flops 2724716544 | bytes 195205968 | solution.py:197
  485.3 9.6 %subtract_exponential_fusion.2 = f32[16,512,512]{1,2,0:T(8,128)} fusion(f32[16,512]{1,0:T(8,128)S(1)} %dynamic-slice_bitcast_fusion.2, pred[512]{0:T(512)(128)(4,1)S(1)} %dynamic-slice_reduce_fusion.5, bf16[2,512,16,64]{1,3,2,0:T(8,128)(2,1)} %get-tuple-element.420, s32[]{:T(128)} %get-tuple-element.403, ...), kind=kOutput, calls=%fused_computation.25.clone.1 | convolution fusion | flops 549453824 | bytes 18908672 | tf_op jit(solution)/shard_map/while/body/eval_jaxpr/qhd,khd->hqk/dot_general | solution.py:49
  494.9 10.5 %multiply_reduce_fusion.7 = (f32[16,512]{1,0:T(8,128)S(1)}, f32[16,512,512]{1,2,0:T(8,128)}) fusion(f32[16,512,512]{1,2,0:T(8,128)} %subtract_exponential_fusion.2, bf16[2,512,16,64]{1,3,2,0:T(8,128)(2,1)S(1)} %copy-done.6, s32[]{:T(128)} %get-tuple-element.403, bf16[2,512,16,64]{1,3,2,0:T(8,128)(2,1)S(1)} %copy-done.2), kind=kOutput, calls=%fused_computation.24.clone.1 | convolution fusion | flops 545251328 | bytes 35685376 | tf_op jit(solution)/shard_map/while/body/eval_jaxpr/qhd,khd->hqk/dot_general | solution.py:74
  505.4 11.9 %multiply_convert_fusion.4 = bf16[16,512,512]{1,2,0:T(8,128)(2,1)S(1)} fusion(f32[16,512,512]{1,2,0:T(8,128)} %subtract_exponential_fusion.2, f32[16,512,512]{1,2,0:T(8,128)} %get-tuple-element.366, f32[16,512]{1,0:T(8,128)S(1)} %get-tuple-element.367), kind=kLoop, calls=%fused_computation.23.clone.1 | loop fusion | flops 12582912 | bytes 41975808 | tf_op jit(solution)/shard_map/while/body/eval_jaxpr/convert_element_type | solution.py:82
  522.8 9.4 %fusion.181 = bf16[2,512,16,64]{1,3,2,0:T(8,128)(2,1)} fusion(bf16[2,512,16,64]{1,3,2,0:T(8,128)(2,1)} %get-tuple-element.406, s32[]{:T(128)} %get-tuple-element.403, f32[16,512,512]{1,2,0:T(8,128)} %subtract_exponential_fusion.2, bf16[2,512,16,64]{1,3,2,0:T(8,128)(2,1)S(1)} %copy-done.2), kind=kOutput, calls=%fused_computation.36.clone.1 | convolution fusion | flops 541589504 | bytes 18875392 | tf_op jit(solution)/shard_map/while/body/eval_jaxpr/hqk,qhd->khd/dot_general | solution.py:75
  532.2 9.6 %subtract_exponential_fusion.2 = f32[16,512,512]{1,2,0:T(8,128)} fusion(f32[16,512]{1,0:T(8,128)S(1)} %dynamic-slice_bitcast_fusion.2, pred[512]{0:T(512)(128)(4,1)S(1)} %dynamic-slice_reduce_fusion.5, bf16[2,512,16,64]{1,3,2,0:T(8,128)(2,1)} %get-tuple-element.420, s32[]{:T(128)} %get-tuple-element.403, ...), kind=kOutput, calls=%fused_computation.25.clone.1 | convolution fusion | flops 549453824 | bytes 18908672 | tf_op jit(solution)/shard_map/while/body/eval_jaxpr/qhd,khd->hqk/dot_general | solution.py:49
  541.9 10.5 %multiply_reduce_fusion.7 = (f32[16,512]{1,0:T(8,128)S(1)}, f32[16,512,512]{1,2,0:T(8,128)}) fusion(f32[16,512,512]{1,2,0:T(8,128)} %subtract_exponential_fusion.2, bf16[2,512,16,64]{1,3,2,0:T(8,128)(2,1)S(1)} %copy-done.6, s32[]{:T(128)} %get-tuple-element.403, bf16[2,512,16,64]{1,3,2,0:T(8,128)(2,1)S(1)} %copy-done.2), kind=kOutput, calls=%fused_computation.24.clone.1 | convolution fusion | flops 545251328 | bytes 35685376 | tf_op jit(solution)/shard_map/while/body/eval_jaxpr/qhd,khd->hqk/dot_general | solution.py:74
  552.3 11.9 %multiply_convert_fusion.4 = bf16[16,512,512]{1,2,0:T(8,128)(2,1)S(1)} fusion(f32[16,512,512]{1,2,0:T(8,128)} %subtract_exponential_fusion.2, f32[16,512,512]{1,2,0:T(8,128)} %get-tuple-element.366, f32[16,512]{1,0:T(8,128)S(1)} %get-tuple-element.367), kind=kLoop, calls=%fused_computation.23.clone.1 | loop fusion | flops 12582912 | bytes 41975808 | tf_op jit(solution)/shard_map/while/body/eval_jaxpr/convert_element_type | solution.py:82
  569.7 9.4 %fusion.181 = bf16[2,512,16,64]{1,3,2,0:T(8,128)(2,1)} fusion(bf16[2,512,16,64]{1,3,2,0:T(8,128)(2,1)} %get-tuple-element.406, s32[]{:T(128)} %get-tuple-element.403, f32[16,512,512]{1,2,0:T(8,128)} %subtract_exponential_fusion.2, bf16[2,512,16,64]{1,3,2,0:T(8,128)(2,1)S(1)} %copy-done.2), kind=kOutput, calls=%fused_computation.36.clone.1 | convolution fusion | flops 541589504 | bytes 18875392 | tf_op jit(solution)/shard_map/while/body/eval_jaxpr/hqk,qhd->khd/dot_general | solution.py:75
  581.1 6.2 copy.112
  589.4 6.2 copy.114
  595.6 5.5 fusion.82
  601.3 6.6 reshape.140
  607.9 4.8 copy.113
  612.6 6.5 reshape.141
  619.2 6.6 reshape.142
  625.8 12.7 %fusion.83 = bf16[1024,1024]{0,1:T(8,128)(2,1)} fusion(f32[1024,1024]{0,1:T(8,128)} %copy-done.17, bf16[3,1024,1024]{2,1,0:T(8,128)(2,1)} %reshape.133, bf16[1,1024,1024]{2,1,0:T(8,128)(2,1)} %reshape.142, bf16[1,1024,1024]{2,1,0:T(8,128)(2,1)} %reshape.141, bf16[1,1024,1024]{2,1,0:T(8,128)(2,1)S(1)} %copy-done.18), kind=kOutput, calls=%fused_computation.106 | convolution fusion | flops 6450839552 | bytes 18874368 | tf_op jit(solution)/shard_map/mte,mde->td/dot_general | solution.py:207
  638.5 4.1 copy.100
  645.2 40.6 %all-reduce = (f32[3,1024]{1,0:T(4,128)}, f32[4096]{0:T(1024)}, f32[1024]{0:T(1024)}, f32[2,1024]{1,0:T(2,128)}, f32[2,1024]{1,0:T(2,128)}) all-reduce(f32[3,1024]{1,0:T(4,128)S(1)} %pad_maximum_fusion, f32[4096]{0:T(1024)S(1)} %copy-done.41, f32[1024]{0:T(1024)S(1)} %get-tuple-element.179, ...), channel_id=1, replica_groups=mesh['dp'=8,'tensor'=4] {'dp','tensor'}, use_global_device_ids=true, to_apply=%region_18.19 | all-reduce | flops 12288 | bytes 98304 | tf_op jit(solution)/shard_map/psum | solution.py:214
  (192 shorter events, 62.2 us)
Async XLA Ops:
  7.2 56.3 %copy-start.19 = (bf16[1024,1024]{1,0:T(8,128)(2,1)S(1)}, bf16[1024,1024]{1,0:T(8,128)(2,1)}, u32[]{:S(2)}) copy-start(bf16[1024,1024]{1,0:T(8,128)(2,1)} %param.18) | copy-start | bytes 6291460
  7.2 58.9 %copy-start.46 = (s32[2,512]{1,0:T(2,128)S(1)}, s32[2,512]{1,0:T(2,128)}, u32[]{:S(2)}) copy-start(s32[2,512]{1,0:T(2,128)} %param.19) | copy-start | bytes 12292
  7.2 59.1 %copy-start.45 = (bf16[4096]{0:T(1024)(128)(2,1)S(1)}, bf16[4096]{0:T(1024)(128)(2,1)}, u32[]{:S(2)}) copy-start(bf16[4096]{0:T(1024)(128)(2,1)} %param.27) | copy-start | bytes 24580
  7.2 59.7 %copy-start.50 = (bf16[1024]{0:T(1024)(128)(2,1)S(1)}, bf16[1024]{0:T(1024)(128)(2,1)}, u32[]{:S(2)}) copy-start(bf16[1024]{0:T(1024)(128)(2,1)} %param.28) | copy-start | bytes 6148
  7.2 54.8 %all-gather.11.cloned.1.call-start = ((), (), s32[]{:S(2)}) async-start(), calls=%async_computation.2 | async-start | bytes 2359296 | tf_op jit(solution)/shard_map/all_gather | solution.py:129
  7.9 105.0 %all-gather.15.cloned.1.call-start = ((), (), s32[]{:S(2)}) async-start(), calls=%async_computation.4 | async-start | bytes 2359296 | tf_op jit(solution)/shard_map/all_gather | solution.py:130
  8.7 161.5 %all-gather.9.cloned.1.call-start = ((), (), s32[]{:S(2)}) async-start(), calls=%async_computation.1 | async-start | bytes 2162688 | tf_op jit(solution)/shard_map/all_gather | solution.py:124
  9.4 231.6 %all-gather.7.cloned.1.call-start = ((), (), s32[]{:S(2)}) async-start(), calls=%async_computation | async-start | bytes 6488064 | tf_op jit(solution)/shard_map/all_gather | solution.py:123
  10.0 342.3 %all-gather.13.cloned.1.call-start = ((), (), s32[]{:S(2)}) async-start(), calls=%async_computation.3 | async-start | bytes 10485760 | tf_op jit(solution)/shard_map/all_gather | solution.py:133
  62.0 307.2 %all-gather.17.cloned.1.call-start = ((), (), s32[]{:S(2)}) async-start(), calls=%async_computation.5 | async-start | bytes 10485760 | tf_op jit(solution)/shard_map/all_gather | solution.py:134
  63.5 8.0 %copy-start.51 = (s32[2]{0:T(128)S(1)}, s32[2]{0:T(128)}, u32[]{:S(2)}) copy-start(s32[2]{0:T(128)} %param.20) | copy-start | bytes 28
  63.5 8.0 %copy-start.42 = (bf16[2,1024]{1,0:T(2,128)(2,1)S(1)}, bf16[2,1024]{1,0:T(2,128)(2,1)}, u32[]{:S(2)}) copy-start(bf16[2,1024]{1,0:T(2,128)(2,1)} %param.21) | copy-start | bytes 12292
  63.5 8.0 %copy-start.43 = (bf16[2,1024]{1,0:T(2,128)(2,1)S(1)}, bf16[2,1024]{1,0:T(2,128)(2,1)}, u32[]{:S(2)}) copy-start(bf16[2,1024]{1,0:T(2,128)(2,1)} %param.29) | copy-start | bytes 12292
  63.5 8.6 %copy-start.44 = (bf16[2,1024]{1,0:T(2,128)(2,1)S(1)}, bf16[2,1024]{1,0:T(2,128)(2,1)}, u32[]{:S(2)}) copy-start(bf16[2,1024]{1,0:T(2,128)(2,1)} %param.30) | copy-start | bytes 12292
  174.4 77.2 %copy-start.22 = (bf16[1024,1024]{0,1:T(8,128)(2,1)S(1)}, bf16[1024,1024]{0,1:T(8,128)(2,1)}, u32[]{:S(2)}) copy-start(bf16[1024,1024]{0,1:T(8,128)(2,1)} %copy.75) | copy-start | bytes 6291460
  341.7 5.2 copy-start
  341.7 5.2 copy-start.24
  341.7 5.2 copy-start.26
  341.7 5.2 copy-start.20
  352.3 16.9 %copy-start.40 = (f32[4096]{0:T(1024)S(1)}, f32[4096]{0:T(1024)}, u32[]{:S(2)}) copy-start(f32[4096]{0:T(1024)} %convert_element_type.124) | copy-start | bytes 49156
  352.3 16.9 %copy-start.47 = (f32[1024]{0:T(1024)S(1)}, f32[1024]{0:T(1024)}, u32[]{:S(2)}) copy-start(f32[1024]{0:T(1024)} %convert_element_type.126) | copy-start | bytes 12292
  369.2 54.2 %copy-start.9 = (bf16[1024,1024]{0,1:T(8,128)(2,1)S(1)}, bf16[1024,1024]{0,1:T(8,128)(2,1)}, u32[]{:S(2)}) copy-start(bf16[1024,1024]{0,1:T(8,128)(2,1)} %copy.85) | copy-start | bytes 6291460
  420.6 26.5 %copy-start.28 = (f32[1024]{0:T(1024)}, f32[1024]{0:T(1024)S(1)}, u32[]{:S(2)}) copy-start(f32[1024]{0:T(1024)S(1)} %broadcast_multiply_fusion.4) | copy-start | bytes 12292
  423.4 23.7 %copy-start.30 = (f32[1024]{0:T(1024)}, f32[1024]{0:T(1024)S(1)}, u32[]{:S(2)}) copy-start(f32[1024]{0:T(1024)S(1)} %add_rsqrt_fusion) | copy-start | bytes 12292
  425.0 22.1 %copy-start.36 = (f32[1024]{0:T(1024)}, f32[1024]{0:T(1024)S(1)}, u32[]{:S(2)}) copy-start(f32[1024]{0:T(1024)S(1)} %get-tuple-element.250) | copy-start | bytes 12292
  425.0 22.1 %copy-start.38 = (f32[1024]{0:T(1024)}, f32[1024]{0:T(1024)S(1)}, u32[]{:S(2)}) copy-start(f32[1024]{0:T(1024)S(1)} %get-tuple-element.251) | copy-start | bytes 12292
  447.1 17.5 %copy-start.12 = (f32[1024,1024]{0,1:T(8,128)S(1)}, f32[1024,1024]{0,1:T(8,128)}, u32[]{:S(2)}) copy-start(f32[1024,1024]{0,1:T(8,128)} %copy-done.11) | copy-start | bytes 12582916
  485.3 9.7 %copy-start.2 = (bf16[2,512,16,64]{1,3,2,0:T(8,128)(2,1)S(1)}, bf16[2,512,16,64]{1,3,2,0:T(8,128)(2,1)}, u32[]{:S(2)}) copy-start(bf16[2,512,16,64]{1,3,2,0:T(8,128)(2,1)} %get-tuple-element.422) | copy-start | bytes 6291460 | tf_op jit(solution)/shard_map/while
  485.3 9.6 %copy-start.6 = (bf16[2,512,16,64]{1,3,2,0:T(8,128)(2,1)S(1)}, bf16[2,512,16,64]{1,3,2,0:T(8,128)(2,1)}, u32[]{:S(2)}) copy-start(bf16[2,512,16,64]{1,3,2,0:T(8,128)(2,1)} %get-tuple-element.423) | copy-start | bytes 6291460 | tf_op jit(solution)/shard_map/while
  505.4 11.9 %copy-start.3 = (bf16[2,512,16,64]{1,3,2,0:T(8,128)(2,1)S(1)}, bf16[2,512,16,64]{1,3,2,0:T(8,128)(2,1)}, u32[]{:S(2)}) copy-start(bf16[2,512,16,64]{1,3,2,0:T(8,128)(2,1)} %get-tuple-element.420) | copy-start | bytes 6291460 | tf_op jit(solution)/shard_map/while
  505.4 11.9 %copy-start.13 = (bf16[2,512,16,64]{1,3,2,0:T(8,128)(2,1)S(1)}, bf16[2,512,16,64]{1,3,2,0:T(8,128)(2,1)}, u32[]{:S(2)}) copy-start(bf16[2,512,16,64]{1,3,2,0:T(8,128)(2,1)} %get-tuple-element.405) | copy-start | bytes 6291460 | tf_op jit(solution)/shard_map/while
  532.2 9.6 %copy-start.2 = (bf16[2,512,16,64]{1,3,2,0:T(8,128)(2,1)S(1)}, bf16[2,512,16,64]{1,3,2,0:T(8,128)(2,1)}, u32[]{:S(2)}) copy-start(bf16[2,512,16,64]{1,3,2,0:T(8,128)(2,1)} %get-tuple-element.422) | copy-start | bytes 6291460 | tf_op jit(solution)/shard_map/while
  532.2 9.6 %copy-start.6 = (bf16[2,512,16,64]{1,3,2,0:T(8,128)(2,1)S(1)}, bf16[2,512,16,64]{1,3,2,0:T(8,128)(2,1)}, u32[]{:S(2)}) copy-start(bf16[2,512,16,64]{1,3,2,0:T(8,128)(2,1)} %get-tuple-element.423) | copy-start | bytes 6291460 | tf_op jit(solution)/shard_map/while
  552.3 11.9 %copy-start.3 = (bf16[2,512,16,64]{1,3,2,0:T(8,128)(2,1)S(1)}, bf16[2,512,16,64]{1,3,2,0:T(8,128)(2,1)}, u32[]{:S(2)}) copy-start(bf16[2,512,16,64]{1,3,2,0:T(8,128)(2,1)} %get-tuple-element.420) | copy-start | bytes 6291460 | tf_op jit(solution)/shard_map/while
  552.3 11.9 %copy-start.13 = (bf16[2,512,16,64]{1,3,2,0:T(8,128)(2,1)S(1)}, bf16[2,512,16,64]{1,3,2,0:T(8,128)(2,1)}, u32[]{:S(2)}) copy-start(bf16[2,512,16,64]{1,3,2,0:T(8,128)(2,1)} %get-tuple-element.405) | copy-start | bytes 6291460 | tf_op jit(solution)/shard_map/while
  587.2 8.3 %copy-start.10 = (bf16[1024,1024]{0,1:T(8,128)(2,1)S(1)}, bf16[1024,1024]{0,1:T(8,128)(2,1)}, u32[]{:S(2)}) copy-start(bf16[1024,1024]{0,1:T(8,128)(2,1)} %copy.85) | copy-start | bytes 6291460
  587.2 8.3 %copy-start.29 = (f32[1024]{0:T(1024)S(1)}, f32[1024]{0:T(1024)}, u32[]{:S(2)}) copy-start(f32[1024]{0:T(1024)} %copy-done.28) | copy-start | bytes 12292
  587.3 8.3 %copy-start.31 = (f32[1024]{0:T(1024)S(1)}, f32[1024]{0:T(1024)}, u32[]{:S(2)}) copy-start(f32[1024]{0:T(1024)} %copy-done.30) | copy-start | bytes 12292
  587.3 8.3 %copy-start.33 = (f32[1,1024]{1,0:T(1,128)S(1)}, f32[1,1024]{1,0:T(1,128)}, u32[]{:S(2)}) copy-start(f32[1,1024]{1,0:T(1,128)} %get-tuple-element.237) | copy-start | bytes 12292
  587.3 8.4 %copy-start.35 = (f32[1,1024]{1,0:T(1,128)S(1)}, f32[1,1024]{1,0:T(1,128)}, u32[]{:S(2)}) copy-start(f32[1,1024]{1,0:T(1,128)} %get-tuple-element.239) | copy-start | bytes 12292
  587.3 8.3 %copy-start.37 = (f32[1024]{0:T(1024)S(1)}, f32[1024]{0:T(1024)}, u32[]{:S(2)}) copy-start(f32[1024]{0:T(1024)} %copy-done.36) | copy-start | bytes 12292
  587.3 8.3 %copy-start.39 = (f32[1024]{0:T(1024)S(1)}, f32[1024]{0:T(1024)}, u32[]{:S(2)}) copy-start(f32[1024]{0:T(1024)} %copy-done.38) | copy-start | bytes 12292
  601.1 6.8 copy-start.15
  619.2 6.6 copy-start.18
  638.5 6.7 copy-start.49
  638.5 6.7 copy-start.48
  638.5 6.7 copy-start.34
  638.5 6.7 copy-start.41
  (18 other events, 57.0 us)
Sparse Core Ops, SparseCore 0:
  10.1 51.7 all-gather.10
  64.0 48.8 all-gather.14
  115.8 54.3 all-gather.8
  172.9 67.9 all-gather.6
  242.4 56.7 all-gather.12
  300.6 58.2 all-gather.16
where the time goes:
time: 704 us; the launch traced here: 693 us
  matrix products  224 us (32%)
  waiting for transfers between devices  219 us (31%)
  local copies, waits for them, and re-layouts  136 us (19%)
  other arithmetic  57.2 us (8%)
  blocking collectives  40.6 us (6%)
  between operations  15.1 us (2%)
    dot_general x3, matrix products, matmul(): return jnp.dot(left_side, right_side, preferred_element_type=jnp.float32)  71.1 us
    all_gather x1, waiting for transfers between devices, per_device(): lax.all_gather(attn_weight, ('dp', 'tensor'), axis=0, tiled=True)  66.6 us
    all_gather x1, waiting for transfers between devices, per_device(): lax.all_gather(out_weight, ('dp', 'tensor'), axis=0, tiled=True)  57.3 us
    all_gather x1, waiting for transfers between devices, per_device(): lax.all_gather(ffn_in_weight, 'dp', axis=0, tiled=True)  51.9 us
    dot_general x3, matrix products, matmul_t(): lax.dot_general(left_side, right_side, (((1,), (1,)), ((), ())), preferre...  42 us
    psum x1, blocking collectives, per_device(): lax.psum((attn_grad, bias_in_grad, bias_out_grad, gain_grad, shift_grad),...  40.6 us
    all_gather x1, waiting for transfers between devices, per_device(): lax.all_gather(ffn_out_weight, 'dp', axis=1, tiled=True)  40.2 us
    another operation x6, local copies, waits for them, and re-layouts, per_device(): stacked = jnp.stack([d_queries, d_keys, d_values])  36.9 us
  transfers between devices with their start and end apart: 6, of which 4 were waited for; matrix products, arithmetic and copies ran while one was open for 20% of the time, Pallas kernels for 0%

commit v1 on v0

v1 whole, which is shorter than its diff:
```python
import functools, math
import jax, jax.numpy as jnp
from jax import lax
from jax.sharding import PartitionSpec as P
from jax.experimental import pallas as pl
from jax.experimental.pallas import tpu as pltpu
MESH = pl.DeviceIdType.MESH

class Gather:
    def __init__(self, groups, sems):
        dp = lax.axis_index("dp"); tn = lax.axis_index("tensor")
        self.z, self.y = dp // 2, dp % 2
        self.x, self.c = tn // 2, tn % 2
        self.inner = (self.z + 1) // 2 % 2
        self.groups = groups
        self.zs, self.zr, self.xs, self.xr, self.ys, self.yr, self.hs, self.hr, self.ds, self.dr, self.loc = sems
        self.todo = []

    def zz(self, e):
        z = self.z
        return [z, z + 1 - 2 * (z % 2), 2 - z // 2, 3 * (1 - z // 2)][e]

    def dev(self, z, y, x, c):
        return (z * 2 + y, x * 2 + c)

    def copy(self, src, dst, ss, rs, dev):
        return pltpu.make_async_remote_copy(src_ref=src, dst_ref=dst, send_sem=ss, recv_sem=rs, device_id=dev, device_id_type=MESH)

    def barrier(self):
        b = pltpu.get_barrier_semaphore()
        z, y, x, c = self.z, self.y, self.x, self.c
        for d in ((z, y, x, 1 - c), (z, y, 1 - x, c), (z, 1 - y, x, c), (self.zz(1), y, x, c)):
            pl.semaphore_signal(b, inc=1, device_id=self.dev(*d), device_id_type=MESH)
        @pl.when(self.inner == 1)
        def _():
            pl.semaphore_signal(b, inc=1, device_id=self.dev(3 - z, y, x, c), device_id_type=MESH)
            pl.semaphore_wait(b, 5)
        @pl.when(self.inner == 0)
        def _():
            pl.semaphore_wait(b, 4)

    def zcopy(self, g, e, k, pair):
        z, y, x, c = self.z, self.y, self.x, self.c
        G = self.groups[g]; zp = self.zz(e)
        view = G["dst"](zp, y, x, c)
        src = G["src"] if e == 0 else view
        to = self.zz(1) if pair else 3 - z
        return self.copy(src, view, self.zs.at[g, k], self.zr.at[g, zp], self.dev(to, y, x, c))

    def zrecv(self, g, e):
        z, y, x, c = self.z, self.y, self.x, self.c
        zp = self.zz(e); view = self.groups[g]["dst"](zp, y, x, c)
        return self.copy(view, view, self.zs.at[g, 0], self.zr.at[g, zp], self.dev(self.zz(1), y, x, c))

    def ncopy(self, g, e, ax):
        z, y, x, c = self.z, self.y, self.x, self.c
        G = self.groups[g]; zp = self.zz(e)
        view = G["dst"](zp, y, x, c)
        src = G["src"] if e == 0 else view
        S, R = (self.xs, self.xr) if ax == "x" else (self.ys, self.yr)
        to = self.dev(z, y, 1 - x, c) if ax == "x" else self.dev(z, 1 - y, x, c)
        return self.copy(src, view, S.at[g, e], R.at[g, e], to)

    def nrecv(self, g, e, ax):
        z, y, x, c = self.z, self.y, self.x, self.c
        view = self.groups[g]["dst"](self.zz(e), y, 1 - x, c) if ax == "x" else self.groups[g]["dst"](self.zz(e), 1 - y, x, c)
        S, R = (self.xs, self.xr) if ax == "x" else (self.ys, self.yr)
        return self.copy(view, view, S.at[g, e], R.at[g, e], self.dev(z, y, x, 1 - c))

    def hcopy(self, g, e, h):
        z, y, x, c = self.z, self.y, self.x, self.c
        G = self.groups[g]; zp = self.zz(e)
        full = G["dst"](zp, 1 - y, x, c) if h == 0 else G["dst"](zp, y, 1 - x, c)
        v = G["half"](full, h)
        to = self.dev(z, y, 1 - x, c) if h == 0 else self.dev(z, 1 - y, x, c)
        return self.copy(v, v, self.hs.at[g, e, h], self.hr.at[g, e, h], to)

    def hrecv(self, g, e, h):
        z, y, x, c = self.z, self.y, self.x, self.c
        G = self.groups[g]
        v = G["half"](G["dst"](self.zz(e), 1 - y, 1 - x, c), h)
        return self.copy(v, v, self.hs.at[g, e, h], self.hr.at[g, e, h], self.dev(z, y, x, 1 - c))

    def dcopy(self, g, e, k, recv=False):
        z, y, x, c = self.z, self.y, self.x, self.c
        G = self.groups[g]; zp = self.zz(e)
        cc = 1 - c if recv else c
        if k == 0: v = G["dst"](zp, y, x, cc)
        elif k == 1: v = G["dst"](zp, y, 1 - x, cc)
        elif k == 2: v = G["dst"](zp, 1 - y, x, cc)
        else: v = G["half"](G["dst"](zp, 1 - y, 1 - x, cc), k - 3)
        src = G["src"] if (e == 0 and k == 0 and not recv) else v
        return self.copy(src, v, self.ds.at[g, e, k], self.dr.at[g, e, k], self.dev(z, y, x, 1 - c))

    def own(self, g):
        G = self.groups[g]
        self.zcopy(g, 0, 0, True).start()
        @pl.when(self.inner == 1)
        def _(): self.zcopy(g, 0, 1, False).start()
        self.ncopy(g, 0, "x").start(); self.ncopy(g, 0, "y").start()
        pltpu.make_async_copy(G["src"], G["dst"](self.z, self.y, self.x, self.c), self.loc.at[g]).start()
        self.dcopy(g, 0, 0).start()

    def avail(self, g, e):
        self.zrecv(g, e).wait_recv()
        @pl.when(self.inner == 1)
        def _(): self.zcopy(g, e, e + 1, e != 1).start()
        self.ncopy(g, e, "x").start(); self.ncopy(g, e, "y").start()
        self.dcopy(g, e, 0).start()

    def near(self, g, e):
        self.nrecv(g, e, "x").wait_recv()
        self.hcopy(g, e, 1).start()
        self.dcopy(g, e, 1).start()
        self.nrecv(g, e, "y").wait_recv()
        self.hcopy(g, e, 0).start()
        self.dcopy(g, e, 2).start()

    def opp(self, g, e):
        for h in (0, 1):
            self.hrecv(g, e, h).wait_recv()
            self.dcopy(g, e, 3 + h).start()

    def partner(self, g, e):
        for k in range(5): self.dcopy(g, e, k, recv=True).wait_recv()

    def local(self, g):
        G = self.groups[g]
        pltpu.make_async_copy(G["src"], G["dst"](self.z, self.y, self.x, self.c), self.loc.at[g]).wait()

    def sent(self, g):
        self.zcopy(g, 0, 0, True).wait_send()
        @pl.when(self.inner == 1)
        def _():
            self.zcopy(g, 0, 1, False).wait_send()
            for e in (1, 2, 3): self.zcopy(g, e, e + 1, e != 1).wait_send()
        for e in range(4):
            self.ncopy(g, e, "x").wait_send(); self.ncopy(g, e, "y").wait_send()
            for h in (0, 1): self.hcopy(g, e, h).wait_send()
            for k in range(5): self.dcopy(g, e, k).wait_send()

    def steps(self, order):
        one = [("own", 0), ("avail", 1), ("near", 0), ("avail", 2), ("near", 1), ("opp", 0), ("avail", 3), ("near", 2), ("opp", 1), ("near", 3), ("opp", 2), ("opp", 3)]
        return one

def sem_shapes(n):
    D = pltpu.SemaphoreType.DMA
    return [D((n, 5)), D((n, 4)), D((n, 4)), D((n, 4)), D((n, 4)), D((n, 4)), D((n, 4, 2)), D((n, 4, 2)), D((n, 4, 5)), D((n, 4, 5)), D((n,))]

def make_groups(qkv, out, w1, w2, gq, go, g1, g2):
    lin = lambda z, y, x, c: ((z * 2 + y) * 2 + x) * 2 + c
    def rows(ref, n):
        return lambda z, y, x, c: ref.at[pl.ds(pl.multiple_of(lin(z, y, x, c) * n, n), n), :]
    def hrows(n):
        return lambda v, h: v.at[pl.ds(h * n, n), :]
    return [
        dict(src=qkv, dst=rows(gq, 96), half=hrows(48)),
        dict(src=out, dst=rows(go, 32), half=hrows(16)),
        dict(src=w1, dst=lambda z, y, x, c: g1.at[x * 2 + c, pl.ds(pl.multiple_of((z * 2 + y) * 128, 128), 128), :], half=hrows(64)),
        dict(src=w2, dst=lambda z, y, x, c: g2.at[x * 2 + c, :, pl.ds(pl.multiple_of((z * 2 + y) * 128, 128), 128)], half=hrows(512)),
    ]

def schedule(n, lag=5):
    one = [("own", 0), ("avail", 1), ("near", 0), ("avail", 2), ("near", 1), ("opp", 0), ("avail", 3), ("near", 2), ("opp", 1), ("near", 3), ("opp", 2), ("opp", 3)]
    ev = []
    for g in range(n):
        for i, s in enumerate(one):
            ev.append((g * 12 + i - (lag if i < 12 - lag else 0) * 0 - g * lag, g, i, s))
    ev.sort(key=lambda t: (t[0], t[1]))
    return [(g, s) for _, g, _, s in ev]

def gather_kernel(lag, qkv, out, w1, w2, gq, go, g1, g2, *sems):
    G = Gather(make_groups(qkv, out, w1, w2, gq, go, g1, g2), sems)
    G.barrier()
    for g, (kind, e) in schedule(4, lag):
        getattr(G, kind)(*((g,) if kind == "own" else (g, e)))
    for g in range(4):
        for e in range(4): G.partner(g, e)
        G.local(g); G.sent(g)

def gather_all(qkv, out, w1, w2, lag=5):
    any_ = pl.BlockSpec(memory_space=pl.ANY); vm = pl.BlockSpec(memory_space=pltpu.VMEM)
    bf = jnp.bfloat16
    S = jax.ShapeDtypeStruct
    return pl.pallas_call(
        functools.partial(gather_kernel, lag),
        out_shape=(S((3072, 1024), bf), S((1024, 1024), bf), S((4, 1024, 1024), bf), S((4, 1024, 1024), bf)),
        in_specs=[vm] * 4, out_specs=(any_,) * 4,
        scratch_shapes=sem_shapes(4),
        compiler_params=pltpu.CompilerParams(collective_id=1, has_side_effects=True),
        name="gather_weights",
    )(qkv, out, w1, w2)
HEADS = 16
HEAD = 64
BF = jnp.bfloat16
F32 = jnp.float32
NN = (((1,), (0,)), ((), ()))
NT = (((1,), (1,)), ((), ()))
TAIL = (0.11962929488154013, 0.12075401780706921, 0.09991309952872984, 0.1285629430504706,
        -0.053686168541539216, 0.20635628544846257, -0.15720471604044917, 0.03567517103968566)


def dot(a, b, dims=NN):
    return lax.dot_general(a, b, dims, preferred_element_type=F32)


def gelu_and_slope(v):
    a = jnp.abs(v)
    t = 1.0 / (1.0 + 0.3 * a)
    e = jnp.exp(-0.5 * v * v)
    r = jnp.full_like(v, TAIL[7])
    for c in TAIL[6::-1]:
        r = r * t + c
    tail = r * t * e
    cdf = jnp.where(v < 0, tail, 1.0 - tail)
    return v * cdf, cdf + v * (e * 0.3989422804014327)


def norm_rows(r):
    mean = jnp.mean(r, axis=-1, keepdims=True)
    cent = r - mean
    inv = lax.rsqrt(jnp.mean(cent * cent, axis=-1, keepdims=True) + 1e-12)
    return cent * inv, inv


def norm_back(u, n, inv, gain):
    s = u * gain
    return inv * (s - jnp.mean(s, axis=-1, keepdims=True) - n * jnp.mean(s * n, axis=-1, keepdims=True))


def colsum(a):
    return jnp.sum(a, axis=0, keepdims=True)


def head_lanes(rows):
    return lax.broadcasted_iota(jnp.int32, (rows, 2 * HEAD), 1) < HEAD


def keep_head(a, h, lanes):
    z = jnp.zeros_like(a)
    return jnp.where(lanes, a, z) if h == 0 else jnp.where(lanes, z, a)


def attend(q, k, v, length):
    seq = q.shape[0]
    lanes = head_lanes(seq)
    ks = k * jnp.asarray(0.125, BF)
    vt = v.T
    valid = lax.broadcasted_iota(jnp.int32, (seq, 1), 0) < length
    bias = jnp.where(valid, 0.0, -1e9)
    outs, totals = [], []
    for h in range(2):
        s = dot(keep_head(ks, h, lanes), q, NT) + bias
        top = jnp.max(s, axis=0, keepdims=True)
        p = jnp.exp(s - top)
        total = jnp.sum(p, axis=0, keepdims=True)
        outs.append(dot(vt[h * HEAD:(h + 1) * HEAD, :], p.astype(BF)) * (1.0 / total))
        totals.append(top + jnp.log(total))
    return jnp.concatenate(outs, axis=0).T.astype(BF), totals


def attend_back(q, k, v, dc, length, totals):
    seq = q.shape[0]
    lanes = head_lanes(seq)
    ks = k * jnp.asarray(0.125, BF)
    kt = ks.T
    valid = lax.broadcasted_iota(jnp.int32, (seq, 1), 0) < length
    bias = jnp.where(valid, 0.0, -1e9)
    dq, dk, dv = [], [], []
    for h in range(2):
        s = dot(keep_head(ks, h, lanes), q, NT) + bias
        p = jnp.exp(s - totals[h])
        dp = dot(keep_head(v, h, lanes), dc, NT)
        row = jnp.sum(p * dp, axis=0, keepdims=True)
        ds = (p * (dp - row)).astype(BF)
        dv.append(dot(p.astype(BF), dc))
        dk.append(dot(ds, q))
        dq.append(dot(kt[h * HEAD:(h + 1) * HEAD, :], ds))
    dq = jnp.concatenate(dq, axis=0).T
    return dq.astype(BF), (jnp.where(lanes, dk[0], dk[1]) * 0.125).astype(BF), jnp.where(lanes, dv[0], dv[1]).astype(BF)


def lane(i, n):
    return pl.ds(pl.multiple_of(i * n, n), n)


def embed(tok, seg, table):
    t = table.astype(F32)
    return tok.astype(F32) + jnp.where(seg == 1, t[1:2, :], t[0:1, :])


def project_qkv(tok, seg, table, bias, wq, qkv, step=256, pump=None):
    for m in range(3):
        def body(i, _):
            r = lane(i, step)
            x = embed(tok[r, :], seg[r, :], table[...]).astype(BF)
            y = dot(x, wq[m * 1024:(m + 1) * 1024, :])
            if m != 1:
                y = y + bias[m // 2:m // 2 + 1, :].astype(F32)
            qkv[m, r, :] = y.astype(BF)
            return 0
        lax.fori_loop(0, tok.shape[0] // step, body, 0)
        if pump: pump()


def attention(qkv, lengths, ctx, totals, seq, s, first, count):
    def body(i, _):
        rows = pl.ds(s * seq, seq)
        cols = lane(i, 128)
        c, t = attend(qkv[0, rows, cols], qkv[1, rows, cols], qkv[2, rows, cols], lengths[s])
        ctx[rows, cols] = c
        for h in range(2):
            totals[pl.ds(s * HEADS + i * 2 + h, 1), :] = t[h]
        return 0
    lax.fori_loop(first, first + count, body, 0)


def middle_rows(r, tok, seg, table, ctx, wo, bias, normed, inv):
    res = embed(tok[r, :], seg[r, :], table[...]) + (dot(ctx[r, :], wo[...]) + bias[2:3, :].astype(F32))
    n, i = norm_rows(res)
    normed[r, :] = n
    inv[r, :] = i


def expand_rows(r, t, w1t, normed, gain, shift, bias1, hidden, slope):
    mid = normed[r, :] * gain[0:1, :].astype(F32) + shift[0:1, :].astype(F32)
    cols = lane(t, 1024)
    v = dot(mid.astype(BF), w1t) + bias1[:, cols].astype(F32)
    h, g = gelu_and_slope(v)
    hidden[r, cols] = h.astype(BF)
    slope[r, cols] = g.astype(BF)


def mlp_kernel(hid, slp, nrm, inv1, cot, w1, w2, wo, gain, shift, bias2,
               out, dfirst, dctx, g_bo, g_b1, g_b2, g_gain, g_shift):
    @pl.when(pl.program_id(0) == 0)
    def _():
        for ref in (g_bo, g_b1, g_b2, g_gain, g_shift):
            ref[...] = jnp.zeros_like(ref)
    ga, sh = gain[...].astype(F32), shift[...].astype(F32)
    n1 = nrm[...]
    res = n1 * ga[0:1] + sh[0:1] + bias2[...].astype(F32)
    for t in range(4):
        res = res + dot(hid[:, t * 1024:(t + 1) * 1024], w2[t])
    n2, inv2 = norm_rows(res)
    out[...] = (n2 * ga[1:2] + sh[1:2]).astype(BF)
    u = cot[...].astype(F32)
    g_gain[1:2, :] += colsum(u * n2)
    g_shift[1:2, :] += colsum(u)
    d2 = norm_back(u, n2, inv2, ga[1:2])
    db = d2.astype(BF)
    g_b2[...] += colsum(db.astype(F32))
    dmid = d2
    for t in range(4):
        c = slice(t * 1024, (t + 1) * 1024)
        dpre = (dot(db, w2[t], NT) * slp[:, c].astype(F32)).astype(BF)
        g_b1[:, c] += colsum(dpre.astype(F32))
        dmid = dmid + dot(dpre, w1[t], NT)
    g_gain[0:1, :] += colsum(dmid * n1)
    g_shift[0:1, :] += colsum(dmid)
    d1 = norm_back(dmid, n1, inv1[...], ga[0:1])
    dfirst[...] = d1
    da = d1.astype(BF)
    g_bo[...] += colsum(da.astype(F32))
    dctx[...] = dot(da, wo[...], NT).astype(BF)


def mlp_call(hid, slp, nrm, inv1, cot, w1, w2, wo, gain, shift, bias2, rows=256):
    tok, d = cot.shape
    ff = hid.shape[1]
    S = jax.ShapeDtypeStruct
    row = lambda n: pl.BlockSpec((rows, n), lambda i: (i, 0))
    one = lambda a: pl.BlockSpec(a.shape, lambda i: (0,) * a.ndim, pipeline_mode=pl.Buffered(1))
    acc = lambda a, b: pl.BlockSpec((a, b), lambda i: (0, 0))
    return pl.pallas_call(
        mlp_kernel,
        grid=(tok // rows,),
        in_specs=[row(ff), row(ff), row(d), row(1), row(d), one(w1), one(w2), one(wo), one(gain), one(shift), one(bias2)],
        out_specs=[row(d), row(d), row(d), acc(1, d), acc(1, ff), acc(1, d), acc(2, d), acc(2, d)],
        out_shape=[S((tok, d), BF), S((tok, d), F32), S((tok, d), BF), S((1, d), F32), S((1, ff), F32), S((1, d), F32), S((2, d), F32), S((2, d), F32)],
        compiler_params=pltpu.CompilerParams(vmem_limit_bytes=62 * 1024 * 1024, dimension_semantics=("arbitrary",)),
        name="mlp",
    )(hid, slp, nrm, inv1, cot, w1, w2, wo, gain, shift, bias2)


def back_kernel(lengths, q, k, v, dc, tot, dfirst, wq, gin, g_q, g_v, grads):
    s, i = pl.program_id(0), pl.program_id(1)
    @pl.when((s == 0) & (i == 0))
    def _():
        g_q[...] = jnp.zeros_like(g_q)
        g_v[...] = jnp.zeros_like(g_v)
    t = [tot[pl.ds(s * HEADS + i * 2 + h, 1), :] for h in range(2)]
    dq, dk, dv = attend_back(q[0], k[0], v[0], dc[...], lengths[s], t)
    cols = lane(i, 128)
    g_q[:, cols] += colsum(dq.astype(F32))
    g_v[:, cols] += colsum(dv.astype(F32))
    for m, a in enumerate((dq, dk, dv)):
        grads[m, :, cols] = a
    @pl.when(i == pl.num_programs(1) - 1)
    def _():
        def body(j, _):
            r = lane(j, 256)
            acc = dfirst[r, :]
            for m in range(3):
                acc = acc + dot(grads[m, r, :], wq[m * 1024:(m + 1) * 1024, :], NT)
            gin[r, :] = acc.astype(BF)
            return 0
        lax.fori_loop(0, gin.shape[0] // 256, body, 0)


def back_call(lengths, qkv, dctx, totals, dfirst, wq, seq):
    tok, d = dctx.shape
    S = jax.ShapeDtypeStruct
    head = lambda m: pl.BlockSpec((1, seq, 128), lambda s, i, ln: (m, s, i))
    return pl.pallas_call(
        back_kernel,
        grid_spec=pltpu.PrefetchScalarGridSpec(
            num_scalar_prefetch=1,
            grid=(tok // seq, d // 128),
            in_specs=[head(0), head(1), head(2), pl.BlockSpec((seq, 128), lambda s, i, ln: (s, i)),
                      pl.BlockSpec(totals.shape, lambda s, i, ln: (0, 0), pipeline_mode=pl.Buffered(1)),
                      pl.BlockSpec((seq, d), lambda s, i, ln: (s, 0)),
                      pl.BlockSpec(wq.shape, lambda s, i, ln: (0, 0), pipeline_mode=pl.Buffered(1))],
            out_specs=[pl.BlockSpec((seq, d), lambda s, i, ln: (s, 0)), pl.BlockSpec((1, d), lambda s, i, ln: (0, 0)), pl.BlockSpec((1, d), lambda s, i, ln: (0, 0))],
            scratch_shapes=[pltpu.VMEM((3, seq, d), BF)],
        ),
        out_shape=[S((tok, d), BF), S((1, d), F32), S((1, d), F32)],
        compiler_params=pltpu.CompilerParams(vmem_limit_bytes=62 * 1024 * 1024, dimension_semantics=("arbitrary", "arbitrary")),
        name="attention_back",
    )(lengths, qkv, qkv, qkv, dctx, totals, dfirst, wq)
def front_kernel(seq, lengths, tok, seg, table, wq, wo, w1, bias, bias1, gain, shift, qkv, totals, normed, inv, hidden, slope, ctx):
    project_qkv(tok, seg, table, bias, wq, qkv)
    n = tok.shape[0]
    for s in range(n // seq):
        attention(qkv, lengths, ctx, totals, seq, s, 0, qkv.shape[2] // 128)
    def mid(i, _):
        middle_rows(lane(i, 256), tok, seg, table, ctx, wo, bias, normed, inv)
        return 0
    lax.fori_loop(0, n // 256, mid, 0)
    def exp(j, _):
        t, i = j // (n // 256), j % (n // 256)
        expand_rows(lane(i, 256), t, w1[t], normed, gain, shift, bias1, hidden, slope)
        return 0
    lax.fori_loop(0, 4 * (n // 256), exp, 0)


def front_call(lengths, tok, seg, table, wq, wo, w1, bias, bias1, gain, shift, seq):
    n, d = tok.shape
    ff = bias1.shape[1]
    S = jax.ShapeDtypeStruct
    vm = pl.BlockSpec(memory_space=pltpu.VMEM)
    return pl.pallas_call(
        functools.partial(front_kernel, seq),
        in_specs=[pl.BlockSpec(memory_space=pltpu.SMEM)] + [vm] * 10,
        out_specs=[vm] * 6,
        out_shape=[S((3, n, d), BF), S((n // seq * HEADS, seq), F32), S((n, d), F32), S((n, 1), F32), S((n, ff), BF), S((n, ff), BF)],
        scratch_shapes=[pltpu.VMEM((n, d), BF)],
        compiler_params=pltpu.CompilerParams(vmem_limit_bytes=64 * 1024 * 1024 - 65536),
        name="front",
    )(lengths, tok, seg, table, wq, wo, w1, bias, bias1, gain, shift)


def per_device(tokens, segments, lengths, type_table, attn_weight, out_weight, ffn_in_weight, ffn_out_weight, attn_bias,
               ffn_bias_in, ffn_bias_out, norm_gain, norm_shift, cotangent):
    n, d = tokens.shape
    seq = segments.shape[1]
    if ffn_in_weight.shape == (128, 1024) and lax.axis_size("dp") == 8 and lax.axis_size("tensor") == 4:
        wq, wo, w1, w2 = gather_all(attn_weight.reshape(-1, d), out_weight.reshape(-1, d), ffn_in_weight, ffn_out_weight, 12)
    else:
        wq = lax.all_gather(attn_weight, ("dp", "tensor"), axis=0, tiled=True).reshape(-1, d)
        wo = lax.all_gather(out_weight, ("dp", "tensor"), axis=0, tiled=True).reshape(-1, d)
        w1 = lax.all_gather(lax.all_gather(ffn_in_weight, "dp", axis=0, tiled=True), "tensor", axis=1, tiled=True)
        w1 = w1.reshape(d, 4, -1).transpose(1, 0, 2)
        w2 = lax.all_gather(lax.all_gather(ffn_out_weight, "dp", axis=1, tiled=True), "tensor", axis=0, tiled=True).reshape(4, -1, d)
    qkv, totals, normed, inv, hidden, slope = front_call(
        lengths, tokens, segments.reshape(-1, 1), type_table, wq, wo, w1, attn_bias, ffn_bias_in[None], norm_gain, norm_shift, seq)
    output, dfirst, dctx, g_bo, g_b1, g_b2, g_gain, g_shift = mlp_call(
        hidden, slope, normed, inv, cotangent, w1, w2, wo, norm_gain, norm_shift, ffn_bias_out[None])
    grad_input, g_q, g_v = back_call(lengths, qkv, dctx, totals, dfirst, wq, seq)
    g_attn = jnp.concatenate([g_q, g_v, g_bo], axis=0)
    sums = lax.psum((g_attn, g_b1[0], g_b2[0], g_gain, g_shift), ("dp", "tensor"))
    return (output, grad_input) + tuple(sums)


def solution(mesh):
    rows = P(("dp", "tensor"), None)
    flat = P(("dp", "tensor"))
    in_specs = (rows, rows, flat, P(), flat, flat, P("dp", "tensor"), P("tensor", "dp"), P(), P(), P(), P(), P(), rows)
    return jax.shard_map(per_device, mesh=mesh, in_specs=in_specs, out_specs=(rows, rows, P(), P(), P(), P(), P()), check_vma=False)
```

time: 704 us -> 326 us (0.46); the launches traced: 693 us -> 325 us
  Pallas kernels: 0 us -> 276 us
  matrix products: 224 us -> 0 us
  waiting for transfers between devices: 219 us -> 0 us
  local copies, waits for them, and re-layouts: 136 us -> 7.51 us
  other arithmetic: 57.2 us -> 0.71 us
  between operations: 15.1 us -> 0.72 us
    pallas_call x0 -> x4, Pallas kernels: none -> 276 us  [the longest x1 112 us: gather_all(): pl.pallas_call(functools.partial(gather_kernel, lag), out_shape=(S((3072,...]
    dot_general x22 -> x0, matrix products: 224 us -> none  [the longest x3 71.1 us: matmul(): return jnp.dot(left_side, right_side, preferred_element_type=jnp.float32)]
    all_gather x6 -> x0, waiting for transfers between devices: 216 us -> none  [the longest x1 66.6 us: per_device(): lax.all_gather(attn_weight, ('dp', 'tensor'), axis=0, tiled=True)]
    another operation x12 -> x0, local copies, waits for them, and re-layouts: 43.3 us -> none  [the longest x6 36.9 us: per_device(): stacked = jnp.stack([d_queries, d_keys, d_values])]
    convert_element_type x7 -> x0, other arithmetic: 33.5 us -> none  [the longest x2 23.7 us: gradient_block(): d_scores = (attn_prob * (d_prob - row_dot)).astype(jnp.bfloat16)]
    reduce_sum x9 -> x0, other arithmetic: 23.5 us -> none  [the longest x2 7.68 us: context_block(): jnp.sum(jnp.exp(masked - row_max), axis=-1, keepdims=True)]
    while x37 -> x0, local copies, waits for them, and re-layouts: 21.2 us -> none  [the longest x4 13.1 us: per_device(): lax.map(partial(context_block, score_scale=score_scale), (query_heads, ke...]
    slice x9 -> x0, local copies, waits for them, and re-layouts: 17.2 us -> none  [the longest x3 9.58 us: per_device(): queries = (projected[0] + bias_attn[0]).astype(jnp.bfloat16)]
  transfers between devices with their start and end apart: 6 -> 0, of which waited for: 4 -> 0; matrix products, arithmetic and copies ran while one was open for 20% -> 0% of each run, Pallas kernels for 0% -> 0%
where the time goes in v1:
time: 326 us; the launch traced here: 325 us
  Pallas kernels  276 us (85%)
  blocking collectives  40.7 us (12%)
  local copies, waits for them, and re-layouts  7.51 us (2%)
    pallas_call x1, Pallas kernels, gather_all(): pl.pallas_call(functools.partial(gather_kernel, lag), out_shape=(S((3072,...  112 us
    pallas_call x1, Pallas kernels, front_call(): pl.pallas_call(functools.partial(front_kernel, seq), in_specs=[pl.BlockSp...  75.9 us
    pallas_call x1, Pallas kernels, mlp_call(): pl.pallas_call(mlp_kernel, grid=(tok // rows,), in_specs=[row(ff), row(ff...  44.2 us
    pallas_call x1, Pallas kernels, back_call(): pl.pallas_call(back_kernel, grid_spec=pltpu.PrefetchScalarGridSpec(num_sc...  43.8 us
    psum x1, blocking collectives, per_device(): lax.psum((g_attn, g_b1[0], g_b2[0], g_gain, g_shift), ('dp', 'tensor'))  40.7 us

profile of v1, /device:TPU:0, one launch (start us, length us, event | category | flops | bytes accessed | tf_op | source)
XLA Modules:
  0.0 325.3 jit_solution(14451091844872759832)
XLA Ops:
  0.6 0.7 copy.22
  1.3 1.3 broadcast_in_dim.7.bias2
  2.6 1.3 broadcast_in_dim.6.bias1
  3.9 1.5 reshape.25.out
  5.4 1.7 reshape.24.qkv
  7.1 1.0 copy.23
  8.1 111.8 %gather_weights.1 = (bf16[3072,1024]{1,0:T(8,128)(2,1)}, bf16[1024,1024]{1,0:T(8,128)(2,1)}, bf16[4,1024,1024]{2,1,0:T(8,128)(2,1)}, bf16[4,1024,1024]{2,1,0:T(8,128)(2,1)}) custom-call(bf16[96,1024]{1,0:T(8,128)(2,1)} %reshape.24.qkv, bf16[32,1024]{1,0:T(8,128)(2,1)} %reshape.25.out, bf16[128,1024]{1,0:T(8,128)(2,1)} %w1.1, bf16[1024,128]{1,0:T(8,128)(2,1)} %w2.1), custom_call_target="tpu_custom_call" | custom-call | tf_op jit(solution)/shard_map/gather_weights/pallas_call | solution.py:185
  119.9 75.9 %front.1 = (bf16[3,1024,1024]{2,1,0:T(8,128)(2,1)}, f32[32,512]{1,0:T(8,128)}, f32[1024,1024]{1,0:T(8,128)}, f32[1024,1]{1,0:T(8,128)}, bf16[1024,4096]{1,0:T(8,128)(2,1)}, /*index=5*/bf16[1024,4096]{1,0:T(8,128)(2,1)}) custom-call(s32[2]{0:T(128)} %lengths.3, bf16[1024,1024]{1,0:T(8,128)(2,1)} %tok.1, s32[1024,1]{1,0:T(8,128)} %bitcast.6, ...), custom_call_target="tpu_custom_call" | custom-call | tf_op jit(solution)/shard_map/front/pallas_call | solution.py:452
  195.8 44.2 %mlp.1 = (bf16[1024,1024]{1,0:T(8,128)(2,1)}, f32[1024,1024]{1,0:T(8,128)}, bf16[1024,1024]{1,0:T(8,128)(2,1)}, f32[1,1024]{1,0:T(1,128)}, f32[1,4096]{1,0:T(1,1...) custom-call(bf16[1024,4096]{1,0:T(8,128)(2,1)} %get-tuple-element.31.hid, ...), custom_call_target="tpu_custom_call" | custom-call | tf_op jit(solution)/shard_map/mlp/pallas_call | solution.py:375
  240.0 0.0 copy-start.3
  240.0 0.0 copy-start
  240.0 0.0 copy-start.1
  240.0 0.0 copy-start.2
  240.1 0.0 copy-start.4
  240.1 43.8 %attention_back.1 = (bf16[1024,1024]{1,0:T(8,128)(2,1)}, f32[1,1024]{1,0:T(1,128)}, f32[1,1024]{1,0:T(1,128)}) custom-call(s32[2]{0:T(128)} %lengths.3, bf16[3,1024,1024]{2,1,0:T(8,128)(2,1)} %get-tuple-element.37.q.k.v, bf16[3,1024,1024]{2,1,0:T(8,128)(2,1)} %get-tuple-element.37.q.k.v, bf16[3,1024,1024]{2,1,0:T(8,128)(2,1)} %get-tuple-element.37.q.k.v, ...), custom_call_target="tpu_custom_call" | custom-call | tf_op jit(solution)/shard_map/attention_back/pallas_call | solution.py:415
  283.8 0.0 copy-done.3
  283.9 0.7 pad_maximum_fusion
  284.6 0.0 copy-done
  284.6 0.0 copy-done.1
  284.6 0.0 copy-done.2
  284.6 0.0 copy-done.4
  284.6 40.7 %all-reduce = (f32[3,1024]{1,0:T(4,128)}, f32[4096]{0:T(1024)}, f32[1024]{0:T(1024)}, f32[2,1024]{1,0:T(2,128)}, f32[2,1024]{1,0:T(2,128)}) all-reduce(f32[3,1024]{1,0:T(4,128)S(1)} %pad_maximum_fusion, f32[4096]{0:T(1024)S(1)} %bitcast.8, f32[1024]{0:T(1024)S(1)} %bitcast.10, ...), channel_id=1, replica_groups=mesh['dp'=8,'tensor'=4] {'dp','tensor'}, use_global_device_ids=true, to_apply=%region_0.0 | all-reduce | flops 12288 | bytes 98304 | tf_op jit(solution)/shard_map/psum | solution.py:481
Async XLA Ops:
  240.0 43.8 %copy-start.3 = (f32[1,1024]{1,0:T(1,128)S(1)}, f32[1,1024]{1,0:T(1,128)}, u32[]{:S(2)}) copy-start(f32[1,1024]{1,0:T(1,128)} %get-tuple-element.44) | copy-start | bytes 12292
  240.0 44.5 %copy-start = (f32[1,4096]{1,0:T(1,128)S(1)}, f32[1,4096]{1,0:T(1,128)}, u32[]{:S(2)}) copy-start(f32[1,4096]{1,0:T(1,128)} %get-tuple-element.45) | copy-start | bytes 49156
  240.0 44.5 %copy-start.1 = (f32[2,1024]{1,0:T(2,128)S(1)}, f32[2,1024]{1,0:T(2,128)}, u32[]{:S(2)}) copy-start(f32[2,1024]{1,0:T(2,128)} %get-tuple-element.47) | copy-start | bytes 24580
  240.0 44.5 %copy-start.2 = (f32[2,1024]{1,0:T(2,128)S(1)}, f32[2,1024]{1,0:T(2,128)}, u32[]{:S(2)}) copy-start(f32[2,1024]{1,0:T(2,128)} %get-tuple-element.48) | copy-start | bytes 24580
  240.1 44.5 %copy-start.4 = (f32[1,1024]{1,0:T(1,128)S(1)}, f32[1,1024]{1,0:T(1,128)}, u32[]{:S(2)}) copy-start(f32[1,1024]{1,0:T(1,128)} %get-tuple-element.46) | copy-start | bytes 12292

commit v2 on v1

--- a/solution.py
+++ b/solution.py
@@ -139,9 +139,10 @@
             for h in (0, 1): self.hcopy(g, e, h).wait_send()
             for k in range(5): self.dcopy(g, e, k).wait_send()
 
-    def steps(self, order):
-        one = [("own", 0), ("avail", 1), ("near", 0), ("avail", 2), ("near", 1), ("opp", 0), ("avail", 3), ("near", 2), ("opp", 1), ("near", 3), ("opp", 2), ("opp", 3)]
-        return one
+    def finish(self, g):
+        for e in range(4):
+            self.partner(g, e)
+        self.local(g)
 
 def sem_shapes(n):
     D = pltpu.SemaphoreType.DMA
@@ -160,36 +161,12 @@
         dict(src=w2, dst=lambda z, y, x, c: g2.at[x * 2 + c, :, pl.ds(pl.multiple_of((z * 2 + y) * 128, 128), 128)], half=hrows(512)),
     ]
 
-def schedule(n, lag=5):
-    one = [("own", 0), ("avail", 1), ("near", 0), ("avail", 2), ("near", 1), ("opp", 0), ("avail", 3), ("near", 2), ("opp", 1), ("near", 3), ("opp", 2), ("opp", 3)]
-    ev = []
-    for g in range(n):
-        for i, s in enumerate(one):
-            ev.append((g * 12 + i - (lag if i < 12 - lag else 0) * 0 - g * lag, g, i, s))
-    ev.sort(key=lambda t: (t[0], t[1]))
-    return [(g, s) for _, g, _, s in ev]
-
-def gather_kernel(lag, qkv, out, w1, w2, gq, go, g1, g2, *sems):
-    G = Gather(make_groups(qkv, out, w1, w2, gq, go, g1, g2), sems)
-    G.barrier()
-    for g, (kind, e) in schedule(4, lag):
-        getattr(G, kind)(*((g,) if kind == "own" else (g, e)))
-    for g in range(4):
-        for e in range(4): G.partner(g, e)
-        G.local(g); G.sent(g)
-
-def gather_all(qkv, out, w1, w2, lag=5):
-    any_ = pl.BlockSpec(memory_space=pl.ANY); vm = pl.BlockSpec(memory_space=pltpu.VMEM)
-    bf = jnp.bfloat16
-    S = jax.ShapeDtypeStruct
-    return pl.pallas_call(
-        functools.partial(gather_kernel, lag),
-        out_shape=(S((3072, 1024), bf), S((1024, 1024), bf), S((4, 1024, 1024), bf), S((4, 1024, 1024), bf)),
-        in_specs=[vm] * 4, out_specs=(any_,) * 4,
-        scratch_shapes=sem_shapes(4),
-        compiler_params=pltpu.CompilerParams(collective_id=1, has_side_effects=True),
-        name="gather_weights",
-    )(qkv, out, w1, w2)
+ORDER = (("own", 0), ("avail", 1), ("near", 0), ("avail", 2), ("near", 1), ("opp", 0), ("avail", 3), ("near", 2), ("opp", 1), ("near", 3), ("opp", 2), ("opp", 3))
+
+
+def schedule(n, lag):
+    ev = sorted(((g * (len(ORDER) - lag) + i, g, s) for g in range(n) for i, s in enumerate(ORDER)), key=lambda t: t[:2])
+    return [(g, s) for _, g, s in ev]
 HEADS = 16
 HEAD = 64
 BF = jnp.bfloat16
@@ -287,32 +264,6 @@
 def embed(tok, seg, table):
     t = table.astype(F32)
     return tok.astype(F32) + jnp.where(seg == 1, t[1:2, :], t[0:1, :])
-
-
-def project_qkv(tok, seg, table, bias, wq, qkv, step=256, pump=None):
-    for m in range(3):
-        def body(i, _):
-            r = lane(i, step)
-            x = embed(tok[r, :], seg[r, :], table[...]).astype(BF)
-            y = dot(x, wq[m * 1024:(m + 1) * 1024, :])
-            if m != 1:
-                y = y + bias[m // 2:m // 2 + 1, :].astype(F32)
-            qkv[m, r, :] = y.astype(BF)
-            return 0
-        lax.fori_loop(0, tok.shape[0] // step, body, 0)
-        if pump: pump()
-
-
-def attention(qkv, lengths, ctx, totals, seq, s, first, count):
-    def body(i, _):
-        rows = pl.ds(s * seq, seq)
-        cols = lane(i, 128)
-        c, t = attend(qkv[0, rows, cols], qkv[1, rows, cols], qkv[2, rows, cols], lengths[s])
-        ctx[rows, cols] = c
-        for h in range(2):
-            totals[pl.ds(s * HEADS + i * 2 + h, 1), :] = t[h]
-        return 0
-    lax.fori_loop(first, first + count, body, 0)
 
 
 def middle_rows(r, tok, seg, table, ctx, wo, bias, normed, inv):
@@ -428,55 +379,213 @@
         compiler_params=pltpu.CompilerParams(vmem_limit_bytes=62 * 1024 * 1024, dimension_semantics=("arbitrary", "arbitrary")),
         name="attention_back",
     )(lengths, qkv, qkv, qkv, dctx, totals, dfirst, wq)
-def front_kernel(seq, lengths, tok, seg, table, wq, wo, w1, bias, bias1, gain, shift, qkv, totals, normed, inv, hidden, slope, ctx):
-    project_qkv(tok, seg, table, bias, wq, qkv)
+LAG = 4
+
+
+class Pump:
+    def __init__(self, G):
+        self.G = G
+        self.ev = schedule(4, LAG) if G else []
+
+    def step(self):
+        g, (kind, e) = self.ev.pop(0)
+        getattr(self.G, kind)(*((g,) if kind == "own" else (g, e)))
+
+    def until(self, g):
+        if self.G:
+            while any(v[0] == g for v in self.ev):
+                self.step()
+            self.G.finish(g)
+
+    def loop(self, count, body, every=1):
+        take = self.ev[:count // every]
+        del self.ev[:count // every]
+
+        def unit(i, _):
+            body(i)
+            for k, (g, (kind, e)) in enumerate(take):
+                @pl.when(i == k * every + every - 1)
+                def _():
+                    getattr(self.G, kind)(*((g,) if kind == "own" else (g, e)))
+            return 0
+        lax.fori_loop(0, count, unit, 0)
+
+
+def front_kernel(seq, gathers, lengths, tok, seg, table, bias, bias1, gain, shift, *refs):
+    if gathers:
+        shards, refs = refs[:4], refs[4:]
+        hq, ho, h1, h2 = refs[:4]
+    else:
+        hq, ho, h1, h2 = refs[:4]
+    qkv_o, totals, normed_o, inv, hidden_o, slope_o = refs[4:10]
+    qkv, ctx, normed, hidden, slope, wq, wo, w1, wsem, osem = refs[10:20]
     n = tok.shape[0]
-    for s in range(n // seq):
-        attention(qkv, lengths, ctx, totals, seq, s, 0, qkv.shape[2] // 128)
-    def mid(i, _):
-        middle_rows(lane(i, 256), tok, seg, table, ctx, wo, bias, normed, inv)
-        return 0
-    lax.fori_loop(0, n // 256, mid, 0)
-    def exp(j, _):
-        t, i = j // (n // 256), j % (n // 256)
-        expand_rows(lane(i, 256), t, w1[t], normed, gain, shift, bias1, hidden, slope)
-        return 0
-    lax.fori_loop(0, 4 * (n // 256), exp, 0)
-
-
-def front_call(lengths, tok, seg, table, wq, wo, w1, bias, bias1, gain, shift, seq):
+    steps = n // 256
+    G = None
+    if gathers:
+        G = Gather(make_groups(*shards, hq, ho, h1, h2), refs[20:])
+        G.barrier()
+    pump = Pump(G)
+    outs = []
+
+    def load(src, dst, k):
+        c = pltpu.make_async_copy(src, dst, wsem.at[k])
+        c.start()
+        return c
+
+    def save(src, dst):
+        c = pltpu.make_async_copy(src, dst, osem.at[len(outs)])
+        c.start()
+        outs.append(c)
+
+    pump.until(0)
+    load(hq, wq, 0).wait()
+    for m in range(3):
+        def project(i, m=m):
+            r = lane(i, 256)
+            x = embed(tok[r, :], seg[r, :], table[...]).astype(BF)
+            y = dot(x, wq[m * 1024:(m + 1) * 1024, :])
+            if m != 1:
+                y = y + bias[m // 2:m // 2 + 1, :].astype(F32)
+            qkv[m, r, :] = y.astype(BF)
+        pump.loop(steps, project, 2)
+        save(qkv.at[m], qkv_o.at[m])
+    heads = qkv.shape[2] // 128
+
+    def attention(j):
+        s, i = j // heads, j % heads
+        rows = pl.ds(pl.multiple_of(s * seq, seq), seq)
+        cols = lane(i, 128)
+        c, t = attend(qkv[0, rows, cols], qkv[1, rows, cols], qkv[2, rows, cols], lengths[s])
+        ctx[rows, cols] = c
+        for h in range(2):
+            totals[pl.ds(s * HEADS + i * 2 + h, 1), :] = t[h]
+    pump.loop(n // seq * heads, attention)
+    pump.until(1)
+    load(ho, wo, 0).wait()
+    pump.loop(steps, lambda i: middle_rows(lane(i, 256), tok, seg, table, ctx, wo, bias, normed, inv))
+    save(normed, normed_o)
+    pump.until(2)
+    tiles = [load(h1.at[t], w1.at[t], t) for t in range(4)]
+    for t in range(4):
+        tiles[t].wait()
+        pump.loop(steps, lambda i, t=t: expand_rows(lane(i, 256), t, w1[t], normed, gain, shift, bias1, hidden, slope), 2)
+        c = pl.ds(t * 1024, 1024)
+        save(hidden.at[:, c], hidden_o.at[:, c])
+        save(slope.at[:, c], slope_o.at[:, c])
+    pump.until(3)
+    for c in outs:
+        c.wait()
+    if gathers:
+        for g in range(4):
+            G.sent(g)
+
+
+def front_call(lengths, tok, seg, table, bias, bias1, gain, shift, weights, seq, gathers):
     n, d = tok.shape
     ff = bias1.shape[1]
     S = jax.ShapeDtypeStruct
     vm = pl.BlockSpec(memory_space=pltpu.VMEM)
+    hbm = pl.BlockSpec(memory_space=pl.ANY)
+    full = [S((3 * d, d), BF), S((d, d), BF), S((4, d, ff // 4), BF), S((4, ff // 4, d), BF)]
+    res = pl.pallas_call(
+        functools.partial(front_kernel, seq, gathers),
+        in_specs=[pl.BlockSpec(memory_space=pltpu.SMEM)] + [vm] * 7 + [vm if gathers else hbm] * 4,
+        out_specs=([hbm] * 4 if gathers else []) + [hbm, vm, hbm, vm, hbm, hbm],
+        out_shape=(full if gathers else []) + [S((3, n, d), BF), S((n // seq * HEADS, seq), F32), S((n, d), F32), S((n, 1), F32), S((n, ff), BF), S((n, ff), BF)],
+        scratch_shapes=[pltpu.VMEM((3, n, d), BF), pltpu.VMEM((n, d), BF), pltpu.VMEM((n, d), F32), pltpu.VMEM((n, ff), BF), pltpu.VMEM((n, ff), BF),
+                        pltpu.VMEM((3 * d, d), BF), pltpu.VMEM((d, d), BF), pltpu.VMEM((4, d, ff // 4), BF),
+                        pltpu.SemaphoreType.DMA((4,)), pltpu.SemaphoreType.DMA((12,))] + (sem_shapes(4) if gathers else []),
+        compiler_params=pltpu.CompilerParams(vmem_limit_bytes=64 * 1024 * 1024 - 65536, **(dict(collective_id=1, has_side_effects=True) if gathers else {})),
+        name="front",
+    )(lengths, tok, seg, table, bias, bias1, gain, shift, *weights)
+    return tuple(weights) + tuple(res) if not gathers else tuple(res)
+
+
+def sum_kernel(g_q, g_v, g_bo, g_b1, g_b2, g_gain, g_shift, o_attn, o_b1, o_b2, o_gain, o_shift, mine, core, square, line, ss, rs):
+    dp = lax.axis_index("dp")
+    tn = lax.axis_index("tensor")
+    z, y, x, c = dp // 2, dp % 2, tn // 2, tn % 2
+    dev = lambda z, y, x, c: (z * 2 + y, x * 2 + c)
+    peers = [dev(z, y, x, 1 - c)]
+    peers += [dev(z, (y + k // 2) % 2, (x + k % 2) % 2, c) for k in (1, 2, 3)]
+    peers += [dev((z + k) % 4, y, x, c) for k in (1, 2, 3)]
+    b = pltpu.get_barrier_semaphore()
+    for p in peers:
+        pl.semaphore_signal(b, inc=1, device_id=p, device_id_type=MESH)
+    mine[0:1, :] = g_q[...]
+    mine[1:2, :] = g_v[...]
+    mine[2:3, :] = g_bo[...]
+    for t in range(4):
+        mine[3 + t:4 + t, :] = g_b1[:, t * 1024:(t + 1) * 1024]
+    mine[7:8, :] = g_b2[...]
+    mine[8:10, :] = g_gain[...]
+    mine[10:12, :] = g_shift[...]
+    mine[12:16, :] = jnp.zeros((4, 1024), F32)
+    pl.semaphore_wait(b, 7)
+
+    def send(k, src, dst, peer):
+        return pltpu.make_async_remote_copy(src_ref=src, dst_ref=dst, send_sem=ss.at[k], recv_sem=rs.at[k], device_id=peer, device_id_type=MESH)
+    first = send(0, mine, core, peers[0])
+    first.start()
+    first.wait()
+    me = y * 2 + x
+    square[me] = mine[...] + core[...]
+    copies = [send(k, square.at[me], square.at[me], peers[k]) for k in (1, 2, 3)]
+    for a in copies:
+        a.start()
+    for a in copies:
+        a.wait()
+    line[z] = (square[0] + square[1]) + (square[2] + square[3])
+    copies = [send(3 + k, line.at[z], line.at[z], peers[3 + k]) for k in (1, 2, 3)]
+    for a in copies:
+        a.start()
+    for a in copies:
+        a.wait()
+    total = (line[0] + line[1]) + (line[2] + line[3])
+    o_attn[...] = total[0:3]
+    o_b1[...] = total[3:7]
+    o_b2[...] = total[7:8]
+    o_gain[...] = total[8:10]
+    o_shift[...] = total[10:12]
+
+
+def sum_call(*parts):
+    S = jax.ShapeDtypeStruct
+    vm = pl.BlockSpec(memory_space=pltpu.VMEM)
     return pl.pallas_call(
-        functools.partial(front_kernel, seq),
-        in_specs=[pl.BlockSpec(memory_space=pltpu.SMEM)] + [vm] * 10,
-        out_specs=[vm] * 6,
-        out_shape=[S((3, n, d), BF), S((n // seq * HEADS, seq), F32), S((n, d), F32), S((n, 1), F32), S((n, ff), BF), S((n, ff), BF)],
-        scratch_shapes=[pltpu.VMEM((n, d), BF)],
-        compiler_params=pltpu.CompilerParams(vmem_limit_bytes=64 * 1024 * 1024 - 65536),
-        name="front",
-    )(lengths, tok, seg, table, wq, wo, w1, bias, bias1, gain, shift)
+        sum_kernel,
+        in_specs=[vm] * 7, out_specs=[vm] * 5,
+        out_shape=[S((3, 1024), F32), S((4, 1024), F32), S((1, 1024), F32), S((2, 1024), F32), S((2, 1024), F32)],
+        scratch_shapes=[pltpu.VMEM((16, 1024), F32), pltpu.VMEM((16, 1024), F32), pltpu.VMEM((4, 16, 1024), F32), pltpu.VMEM((4, 16, 1024), F32),
+                        pltpu.SemaphoreType.DMA((7,)), pltpu.SemaphoreType.DMA((7,))],
+        compiler_params=pltpu.CompilerParams(collective_id=2, has_side_effects=True),
+        name="sum_gradients",
+    )(*parts)
 
 
 def per_device(tokens, segments, lengths, type_table, attn_weight, out_weight, ffn_in_weight, ffn_out_weight, attn_bias,
                ffn_bias_in, ffn_bias_out, norm_gain, norm_shift, cotangent):
     n, d = tokens.shape
     seq = segments.shape[1]
-    if ffn_in_weight.shape == (128, 1024) and lax.axis_size("dp") == 8 and lax.axis_size("tensor") == 4:
-        wq, wo, w1, w2 = gather_all(attn_weight.reshape(-1, d), out_weight.reshape(-1, d), ffn_in_weight, ffn_out_weight, 12)
+    kernels = lax.axis_size("dp") == 8 and lax.axis_size("tensor") == 4
+    if kernels:
+        weights = attn_weight.reshape(-1, d), out_weight.reshape(-1, d), ffn_in_weight, ffn_out_weight
     else:
         wq = lax.all_gather(attn_weight, ("dp", "tensor"), axis=0, tiled=True).reshape(-1, d)
         wo = lax.all_gather(out_weight, ("dp", "tensor"), axis=0, tiled=True).reshape(-1, d)
         w1 = lax.all_gather(lax.all_gather(ffn_in_weight, "dp", axis=0, tiled=True), "tensor", axis=1, tiled=True)
         w1 = w1.reshape(d, 4, -1).transpose(1, 0, 2)
         w2 = lax.all_gather(lax.all_gather(ffn_out_weight, "dp", axis=1, tiled=True), "tensor", axis=0, tiled=True).reshape(4, -1, d)
-    qkv, totals, normed, inv, hidden, slope = front_call(
-        lengths, tokens, segments.reshape(-1, 1), type_table, wq, wo, w1, attn_bias, ffn_bias_in[None], norm_gain, norm_shift, seq)
+        weights = wq, wo, w1, w2
+    wq, wo, w1, w2, qkv, totals, normed, inv, hidden, slope = front_call(
+        lengths, tokens, segments.reshape(-1, 1), type_table, attn_bias, ffn_bias_in[None], norm_gain, norm_shift, weights, seq, kernels)
     output, dfirst, dctx, g_bo, g_b1, g_b2, g_gain, g_shift = mlp_call(
         hidden, slope, normed, inv, cotangent, w1, w2, wo, norm_gain, norm_shift, ffn_bias_out[None])
     grad_input, g_q, g_v = back_call(lengths, qkv, dctx, totals, dfirst, wq, seq)
+    if kernels:
+        g_attn, g_b1, g_b2, g_gain, g_shift = sum_call(g_q, g_v, g_bo, g_b1, g_b2, g_gain, g_shift)
+        return output, grad_input, g_attn, g_b1.reshape(-1), g_b2[0], g_gain, g_shift
     g_attn = jnp.concatenate([g_q, g_v, g_bo], axis=0)
     sums = lax.psum((g_attn, g_b1[0], g_b2[0], g_gain, g_shift), ("dp", "tensor"))
     return (output, grad_input) + tuple(sums)

time: 326 us -> 269 us (0.83)
  blocking collectives: 40.7 us -> 0 us
  Pallas kernels: 276 us -> 253 us
  local copies, waits for them, and re-layouts: 7.51 us -> 14 us
    psum x1 -> x0, blocking collectives: 40.7 us -> none  [per_device(): lax.psum((g_attn, g_b1[0], g_b2[0], g_gain, g_shift), ('dp', 'tensor'))]
    pallas_call x2, Pallas kernels: 188 us -> 166 us  [the longest x1 148 us: front_call(): pl.pallas_call(functools.partial(front_kernel, seq, gathers), in_specs=[p...]
    unnamed x12 -> x7, local copies, waits for them, and re-layouts: 1.75 us -> 8.22 us
where the time goes in v2:
time: 269 us; the launch traced here: 268 us
  Pallas kernels  253 us (94%)
  local copies, waits for them, and re-layouts  14 us (5%)
    pallas_call x1, Pallas kernels, front_call(): pl.pallas_call(functools.partial(front_kernel, seq, gathers), in_specs=[p...  148 us
    pallas_call x1, Pallas kernels, mlp_call(): pl.pallas_call(mlp_kernel, grid=(tok // rows,), in_specs=[row(ff), row(ff...  44.2 us
    pallas_call x1, Pallas kernels, back_call(): pl.pallas_call(back_kernel, grid_spec=pltpu.PrefetchScalarGridSpec(num_sc...  43.7 us
    pallas_call x1, Pallas kernels, sum_call(): pl.pallas_call(sum_kernel, in_specs=[vm] * 7, out_specs=[vm] * 5, out_sha...  17.4 us
    unnamed x7, local copies, waits for them, and re-layouts  8.22 us

profile of v2, /device:TPU:0, one launch (start us, length us, event | category | flops | bytes accessed | tf_op | source)
XLA Modules:
  0.0 268.1 jit_solution(5246889235694123624)
XLA Ops:
  0.6 0.7 copy.22
  1.3 1.3 broadcast_in_dim.7.bias2
  2.6 1.3 broadcast_in_dim.6.bias1
  3.9 1.5 reshape.28.refs_1_
  5.4 1.7 reshape.27.refs_0_
  7.1 1.0 copy.23
  8.1 148.1 %front.1 = (bf16[3072,1024]{1,0:T(8,128)(2,1)}, bf16[1024,1024]{1,0:T(8,128)(2,1)}, bf16[4,1024,1024]{2,1,0:T(8,128)(2,1)}, bf16[4,1024,1024]{2,1,0:T(8,128)(2,1...) custom-call(s32[2]{0:T(128)} %lengths.3, ...), custom_call_target="tpu_custom_call" | custom-call | tf_op jit(solution)/shard_map/front/pallas_call | solution.py:491
  156.2 44.2 %mlp.1 = (bf16[1024,1024]{1,0:T(8,128)(2,1)}, f32[1024,1024]{1,0:T(8,128)}, bf16[1024,1024]{1,0:T(8,128)(2,1)}, f32[1,1024]{1,0:T(1,128)}, f32[1,4096]{1,0:T(1,1...) custom-call(bf16[1024,4096]{1,0:T(8,128)(2,1)} %get-tuple-element.33.hid, ...), custom_call_target="tpu_custom_call" | custom-call | tf_op jit(solution)/shard_map/mlp/pallas_call | solution.py:326
  200.5 43.7 %attention_back.1 = (bf16[1024,1024]{1,0:T(8,128)(2,1)}, f32[1,1024]{1,0:T(1,128)}, f32[1,1024]{1,0:T(1,128)}) custom-call(s32[2]{0:T(128)} %lengths.3, bf16[3,1024,1024]{2,1,0:T(8,128)(2,1)} %get-tuple-element.41.q.k.v, bf16[3,1024,1024]{2,1,0:T(8,128)(2,1)} %get-tuple-element.41.q.k.v, bf16[3,1024,1024]{2,1,0:T(8,128)(2,1)} %get-tuple-element.41.q.k.v, ...), custom_call_target="tpu_custom_call" | custom-call | tf_op jit(solution)/shard_map/attention_back/pallas_call | solution.py:366
  244.1 17.4 %sum_gradients.1 = (f32[3,1024]{1,0:T(4,128)}, f32[4,1024]{1,0:T(4,128)}, f32[1,1024]{1,0:T(1,128)}, f32[2,1024]{1,0:T(2,128)}, f32[2,1024]{1,0:T(2,128)}) custom-call(f32[1,1024]{1,0:T(1,128)} %get-tuple-element.47.g_q, f32[1,1024]{1,0:T(1,128)} %get-tuple-element.48.g_v, f32[1,1024]{1,0:T(1,128)} %get-tuple-element.49.g_bo, ...), custom_call_target="tpu_custom_call" | custom-call | tf_op jit(solution)/shard_map/sum_gradients/pallas_call | solution.py:556
  261.6 1.3 copy.26
  262.9 1.3 copy.31
  264.2 1.3 copy.32
  265.5 1.3 copy.33
  266.8 1.3 copy.34
